TPU v7x, 256 devices: a whole 4x4x8 slice. The times are simulated.
256 devices in a mesh: tm: 32 (over x_lo, z, core), space: 8 (over y, x_hi).
Axes of the slice: x: 4 (x_hi: 2, x_lo: 2; x = x_hi * 2 + x_lo), y: 4, z: 8, core: 2. Of those that a mesh axis runs over, the one named last changes fastest.
Arguments:
- forcing: float32 [32, 32, 128, 128], P('tm', 'space'), may hold values from -6 to 6
- initial: float32 [32, 128, 128], P('space'), may hold values from -6 to 6
- coupling: float32 [32, 128, 128], P('space'), may hold values from 0.3 to 3
- velocity: float32 [3, 32, 128, 128], P(None, 'space'), may hold values from -0.9 to 0.9
Outputs:
- iterate: float32 [32, 32, 128, 128], P('tm', 'space')
All inputs are finite; a program needn't handle non-finite values.
Results may differ from a plain program's by a relative error of at most 0.0003.
Values sent between devices are 32-bit elements; how exact they have to be, the bound alone decides.
A program may use at most 64 MiB of HBM per device.

v0:
```python
import math

import jax
import jax.numpy as jnp
from jax import lax
from jax.sharding import PartitionSpec as P

ITERS = 2
SWEEPS = 8


wrap_alpha = 0.1


def passed_along(array, axis, by):
    size = lax.axis_size(axis)
    pairs = [(i, i + by) for i in range(size) if 0 <= i + by < size]
    return lax.ppermute(array, axis, pairs)


def with_halo(block, sides, width):
    for axis, dim in sides:
        count = lax.axis_size(axis)
        forward = [(i, i + 1) for i in range(count - 1)]
        backward = [(target, source) for source, target in forward]
        low = lax.ppermute(
            lax.slice_in_dim(block, block.shape[dim] - width, None, axis=dim), axis, forward
        )
        high = lax.ppermute(lax.slice_in_dim(block, 0, width, axis=dim), axis, backward)
        block = jnp.concatenate([low, block, high], axis=dim)
    return block


def coupled(extended, coupling, advect):
    total = (coupling - advect[0]) * extended[..., 2:, 1:-1, 1:-1] + (
        coupling + advect[0]
    ) * extended[..., :-2, 1:-1, 1:-1]
    total = (
        total
        + (coupling - advect[1]) * extended[..., 1:-1, 2:, 1:-1]
        + (coupling + advect[1]) * extended[..., 1:-1, :-2, 1:-1]
    )
    total = (
        total
        + (coupling - advect[2]) * extended[..., 1:-1, 1:-1, 2:]
        + (coupling + advect[2]) * extended[..., 1:-1, 1:-1, :-2]
    )
    return total


def tables(total_steps):
    indices = jnp.arange(total_steps, dtype=jnp.int32)
    products = indices[:, None] * indices[None, :] % total_steps
    angles = products.astype(jnp.float32) * (2.0 * math.pi / total_steps)
    return (jnp.cos(angles), jnp.sin(angles))


def matmul(table, columns):
    return jnp.dot(
        table, columns, preferred_element_type=jnp.float32, precision=lax.Precision.HIGHEST
    )


def jacobi(spectrum, coupling, advect, frequency, total_steps, extend):
    radius = math.exp(math.log(wrap_alpha) / total_steps)
    angles = (frequency * (2.0 * math.pi / total_steps))[:, None, None, None]
    diag_re = 1.0 + 6.0 * coupling - radius * jnp.cos(angles)
    diag_im = radius * jnp.sin(angles) + jnp.zeros_like(diag_re)
    modulus = diag_re * diag_re + diag_im * diag_im
    source_re = spectrum[0]
    source_im = spectrum[1]
    value_re = (source_re * diag_re + source_im * diag_im) / modulus
    value_im = (source_im * diag_re - source_re * diag_im) / modulus
    for sweep in range(SWEEPS):
        extended = extend(jnp.stack([value_re, value_im]))
        summed = coupled(extended, coupling, advect)
        sum_re = source_re + summed[0]
        sum_im = source_im + summed[1]
        value_re = (sum_re * diag_re + sum_im * diag_im) / modulus
        value_im = (sum_im * diag_re - sum_re * diag_im) / modulus
    return jnp.stack([value_re, value_im])


def body(forcing, initial, coupling, velocity):
    local_steps = forcing.shape[0]
    groups = lax.axis_size("tm")
    total_steps = local_steps * groups
    time_index = lax.axis_index("tm")
    advect = coupling[None] * velocity
    cosine, sine_table = tables(total_steps)
    global_steps = (time_index * local_steps + jnp.arange(local_steps, dtype=jnp.int32)).astype(
        jnp.float32
    )
    time_weight = jnp.exp(math.log(wrap_alpha) * global_steps / total_steps)[:, None, None, None]
    iterate = jnp.broadcast_to(initial, forcing.shape)

    def forward(piece):
        columns = piece.reshape(piece.shape[0], -1)
        spec_re = matmul(cosine, columns)
        spec_im = -matmul(sine_table, columns)
        return jnp.stack([spec_re, spec_im]).reshape((2,) + piece.shape)

    for repeat in range(ITERS):
        before = passed_along(iterate[-1], "tm", 1)
        before = jnp.where(time_index == 0, initial, before)
        previous = jnp.concatenate([before[None], iterate[:-1]], axis=0)
        extended = with_halo(iterate, (("space", 1),), 1)
        extended = jnp.pad(extended, ((0, 0), (0, 0), (1, 1), (1, 1)))
        residual = (
            forcing
            - ((1.0 + 6.0 * coupling) * iterate - coupled(extended, coupling, advect))
            + previous
        )
        scaled = residual * time_weight
        spectrum = forward(lax.all_to_all(scaled, "tm", split_axis=2, concat_axis=0, tiled=True))
        blocked = lax.all_to_all(spectrum, "tm", split_axis=1, concat_axis=3, tiled=True)
        frequency = (time_index * local_steps + jnp.arange(local_steps, dtype=jnp.int32)).astype(
            jnp.float32
        )

        def extend_narrow(field):
            grown = with_halo(field, (("space", 2),), 1)
            return jnp.pad(grown, ((0, 0), (0, 0), (0, 0), (1, 1), (1, 1)))

        solved = jacobi(blocked, coupling, advect, frequency, total_steps, extend_narrow)
        spectrum_out = lax.all_to_all(solved, "tm", split_axis=3, concat_axis=1, tiled=True)
        inverse_part = (
            matmul(cosine, spectrum_out[0].reshape(total_steps, -1))
            - matmul(sine_table, spectrum_out[1].reshape(total_steps, -1))
        ) / total_steps
        inverse_part = inverse_part.reshape(spectrum_out.shape[1:])
        correction = lax.all_to_all(inverse_part, "tm", split_axis=0, concat_axis=2, tiled=True)
        iterate = iterate + correction / time_weight
    return iterate


def solution(mesh):
    return jax.shard_map(
        body,
        mesh=mesh,
        in_specs=(
            P("tm", "space", None, None),
            P("space", None, None),
            P("space", None, None),
            P(None, "space", None, None),
        ),
        out_specs=P("tm", "space", None, None),
        check_vma=False,
    )
```

profile of v0, /device:TPU:1, one launch (start us, length us, event | category | flops | bytes accessed | tf_op | source)
XLA Modules:
  0.0 412.8 jit_solution(2758898174623580180)
XLA Ops:
  0.0 5.0 %collective-permute-start.2 = (f32[4,128,128]{2,1,0:T(8,128)}, f32[4,128,128]{2,1,0:T(8,128)S(1)}, u32[]{:S(2)}, u32[]{:S(2)}) collective-permute-start(f32[4,128,128]{2,1,0:T(8,128)} %param.5), channel_id=1, source_target_pairs={{0,8},{8,16},{16,24},{24,32},{32,40},{40,48},{48,56},{56,64},{64,7... | collective-permute-start | bytes 786440 | tf_op jit(solution)/shard_map/ppermute | solution.py:18
  6.0 4.7 %collective-permute-start.1 = (f32[1,1,128,128]{3,2,1,0:T(8,128)S(1)}, f32[1,1,128,128]{3,2,1,0:T(8,128)S(1)}, u32[]{:S(2)}, u32[]{:S(2)}) collective-permute-start(f32[1,1,128,128]{3,2,1,0:T(8,128)S(1)} %get-tuple-element.90), channel_id=1, source_target_pairs={{0,1},{1,2},{2,3},{3,4},{4,5},{5,6},{6,7},{8,9},{9,10},{10,11},{11... | collective-permute-start | bytes 196616 | tf_op jit(solution)/shard_map/ppermute | solution.py:26
  13.3 4.0 collective-permute-done
  18.2 20.4 %all_to_all.108 = f32[1,4,128,128]{3,1,0,2:T(4,128)S(1)} all-to-all(f32[1,4,128,128]{3,1,0,2:T(4,128)S(1)} %copy.21), channel_id=1, replica_groups=mesh['tm'=32,'space'=8] {'tm'}, dimensions={2} | all-to-all | bytes 524288 | tf_op jit(solution)/shard_map/all_to_all | solution.py:115
  41.4 5.4 %all-to-all-start.1 = ((f32[2,32,4,4,128]{4,3,2,0,1:T(4,128)}), f32[2,32,4,4,128]{4,3,2,0,1:T(4,128)S(1)}, u32[]{:S(2)}, u32[]{:S(2)}) async-start(f32[2,32,4,4,128]{4,3,2,0,1:T(4,128)} %copy.25), calls=%async_computation.1 | async-start | bytes 1048576 | tf_op jit(solution)/shard_map/all_to_all | solution.py:116
  46.9 16.5 %all-to-all-done.1 = f32[2,32,4,4,128]{4,3,2,0,1:T(4,128)S(1)} async-done(((f32[2,32,4,4,128]{4,3,2,0,1:T(4,128)}), f32[2,32,4,4,128]{4,3,2,0,1:T(4,128)S(1)}, u32[]{:S(2)}, u32[]{:S(2)}) %all-to-all-start.1) | async-done | bytes 524320 | tf_op jit(solution)/shard_map/all_to_all | solution.py:116
  63.8 5.5 %collective-permute-start.4 = (f32[2,1,1,128,128]{4,3,2,1,0:T(8,128)S(1)}, f32[2,1,1,128,128]{4,3,2,1,0:T(8,128)S(1)}, u32[]{:S(2)}, u32[]{:S(2)}) collective-permute-start(f32[2,1,1,128,128]{4,3,2,1,0:T(8,128)S(1)} %get-tuple-element.84), channel_id=1, source_target_pairs={{0,1},{1,2},{2,3},{3,4},{4,5},{5,6},{6,7},{8,9},{9,10},{10,11},{11... | collective-permute-start | bytes 393224 | tf_op jit(solution)/shard_map/ppermute | solution.py:26
  71.3 5.3 %collective-permute-done.3 = f32[2,1,1,128,128]{4,3,2,1,0:T(8,128)S(1)} collective-permute-done((f32[2,1,1,128,128]{4,3,2,1,0:T(8,128)S(1)}, f32[2,1,1,128,128]{4,3,2,1,0:T(8,128)S(1)}, u32[]{:S(2)}, u32[]{:S(2)}) %collective-permute-start.3) | collective-permute-done | bytes 131104 | tf_op jit(solution)/shard_map/ppermute | solution.py:29
  77.8 4.2 %collective-permute-start.6 = (f32[2,1,1,128,128]{4,3,2,1,0:T(8,128)S(1)}, f32[2,1,1,128,128]{4,3,2,1,0:T(8,128)S(1)}, u32[]{:S(2)}, u32[]{:S(2)}) collective-permute-start(f32[2,1,1,128,128]{4,3,2,1,0:T(8,128)S(1)} %get-tuple-element.82), channel_id=1, source_target_pairs={{0,1},{1,2},{2,3},{3,4},{4,5},{5,6},{6,7},{8,9},{9,10},{10,11},{11... | collective-permute-start | bytes 393224 | tf_op jit(solution)/shard_map/ppermute | solution.py:26
  83.9 5.9 %collective-permute-done.5 = f32[2,1,1,128,128]{4,3,2,1,0:T(8,128)S(1)} collective-permute-done((f32[2,1,1,128,128]{4,3,2,1,0:T(8,128)S(1)}, f32[2,1,1,128,128]{4,3,2,1,0:T(8,128)S(1)}, u32[]{:S(2)}, u32[]{:S(2)}) %collective-permute-start.5) | collective-permute-done | bytes 131104 | tf_op jit(solution)/shard_map/ppermute | solution.py:29
  91.1 4.7 %collective-permute-start.8 = (f32[2,1,1,128,128]{4,3,2,1,0:T(8,128)S(1)}, f32[2,1,1,128,128]{4,3,2,1,0:T(8,128)S(1)}, u32[]{:S(2)}, u32[]{:S(2)}) collective-permute-start(f32[2,1,1,128,128]{4,3,2,1,0:T(8,128)S(1)} %get-tuple-element.80), channel_id=1, source_target_pairs={{0,1},{1,2},{2,3},{3,4},{4,5},{5,6},{6,7},{8,9},{9,10},{10,11},{11... | collective-permute-start | bytes 393224 | tf_op jit(solution)/shard_map/ppermute | solution.py:26
  97.8 6.7 %collective-permute-done.7 = f32[2,1,1,128,128]{4,3,2,1,0:T(8,128)S(1)} collective-permute-done((f32[2,1,1,128,128]{4,3,2,1,0:T(8,128)S(1)}, f32[2,1,1,128,128]{4,3,2,1,0:T(8,128)S(1)}, u32[]{:S(2)}, u32[]{:S(2)}) %collective-permute-start.7) | collective-permute-done | bytes 131104 | tf_op jit(solution)/shard_map/ppermute | solution.py:29
  105.7 4.6 %collective-permute-start.10 = (f32[2,1,1,128,128]{4,3,2,1,0:T(8,128)S(1)}, f32[2,1,1,128,128]{4,3,2,1,0:T(8,128)S(1)}, u32[]{:S(2)}, u32[]{:S(2)}) collective-permute-start(f32[2,1,1,128,128]{4,3,2,1,0:T(8,128)S(1)} %get-tuple-element.78), channel_id=1, source_target_pairs={{0,1},{1,2},{2,3},{3,4},{4,5},{5,6},{6,7},{8,9},{9,10},{10,11},{11... | collective-permute-start | bytes 393224 | tf_op jit(solution)/shard_map/ppermute | solution.py:26
  112.2 6.0 %collective-permute-done.9 = f32[2,1,1,128,128]{4,3,2,1,0:T(8,128)S(1)} collective-permute-done((f32[2,1,1,128,128]{4,3,2,1,0:T(8,128)S(1)}, f32[2,1,1,128,128]{4,3,2,1,0:T(8,128)S(1)}, u32[]{:S(2)}, u32[]{:S(2)}) %collective-permute-start.9) | collective-permute-done | bytes 131104 | tf_op jit(solution)/shard_map/ppermute | solution.py:29
  119.5 4.7 %collective-permute-start.12 = (f32[2,1,1,128,128]{4,3,2,1,0:T(8,128)S(1)}, f32[2,1,1,128,128]{4,3,2,1,0:T(8,128)S(1)}, u32[]{:S(2)}, u32[]{:S(2)}) collective-permute-start(f32[2,1,1,128,128]{4,3,2,1,0:T(8,128)S(1)} %get-tuple-element.76), channel_id=1, source_target_pairs={{0,1},{1,2},{2,3},{3,4},{4,5},{5,6},{6,7},{8,9},{9,10},{10,11},{11... | collective-permute-start | bytes 393224 | tf_op jit(solution)/shard_map/ppermute | solution.py:26
  126.1 6.7 %collective-permute-done.11 = f32[2,1,1,128,128]{4,3,2,1,0:T(8,128)S(1)} collective-permute-done((f32[2,1,1,128,128]{4,3,2,1,0:T(8,128)S(1)}, f32[2,1,1,128,128]{4,3,2,1,0:T(8,128)S(1)}, u32[]{:S(2)}, u32[]{:S(2)}) %collective-permute-start.11) | collective-permute-done | bytes 131104 | tf_op jit(solution)/shard_map/ppermute | solution.py:29
  137.4 5.3 %collective-permute-done.13 = f32[2,1,1,128,128]{4,3,2,1,0:T(8,128)S(1)} collective-permute-done((f32[2,1,1,128,128]{4,3,2,1,0:T(8,128)S(1)}, f32[2,1,1,128,128]{4,3,2,1,0:T(8,128)S(1)}, u32[]{:S(2)}, u32[]{:S(2)}) %collective-permute-start.13) | collective-permute-done | bytes 131104 | tf_op jit(solution)/shard_map/ppermute | solution.py:29
  143.9 2.8 collective-permute-start.16
  148.7 5.3 %collective-permute-done.15 = f32[2,1,1,128,128]{4,3,2,1,0:T(8,128)S(1)} collective-permute-done((f32[2,1,1,128,128]{4,3,2,1,0:T(8,128)S(1)}, f32[2,1,1,128,128]{4,3,2,1,0:T(8,128)S(1)}, u32[]{:S(2)}, u32[]{:S(2)}) %collective-permute-start.15) | collective-permute-done | bytes 131104 | tf_op jit(solution)/shard_map/ppermute | solution.py:29
  155.2 2.8 collective-permute-start.18
  160.0 5.3 %collective-permute-done.17 = f32[2,1,1,128,128]{4,3,2,1,0:T(8,128)S(1)} collective-permute-done((f32[2,1,1,128,128]{4,3,2,1,0:T(8,128)S(1)}, f32[2,1,1,128,128]{4,3,2,1,0:T(8,128)S(1)}, u32[]{:S(2)}, u32[]{:S(2)}) %collective-permute-start.17) | collective-permute-done | bytes 131104 | tf_op jit(solution)/shard_map/ppermute | solution.py:29
  166.9 30.9 %all_to_all.109 = f32[2,1,4,128,128]{4,2,1,0,3:T(4,128)S(1)} all-to-all(f32[2,1,4,128,128]{4,2,1,0,3:T(4,128)S(1)} %copy.28), channel_id=1, replica_groups=mesh['tm'=32,'space'=8] {'tm'}, dimensions={3} | all-to-all | bytes 1048576 | tf_op jit(solution)/shard_map/all_to_all | solution.py:126
  199.2 16.6 %all_to_all.110 = f32[32,4,4,128]{3,2,1,0:T(4,128)S(1)} all-to-all(f32[32,4,4,128]{3,2,1,0:T(4,128)S(1)} %reshape.488), channel_id=1, replica_groups=mesh['tm'=32,'space'=8] {'tm'}, dimensions={0} | all-to-all | bytes 524288 | tf_op jit(solution)/shard_map/all_to_all | solution.py:132
  216.0 3.9 collective-permute-start.21
  219.9 3.0 collective-permute-start.20
  224.2 2.1 collective-permute-done.20
  226.3 3.6 collective-permute-done.19
  230.8 14.9 %all_to_all.111 = f32[1,4,128,128]{3,1,0,2:T(4,128)S(1)} all-to-all(f32[1,4,128,128]{3,1,0,2:T(4,128)S(1)} %copy.31), channel_id=1, replica_groups=mesh['tm'=32,'space'=8] {'tm'}, dimensions={2} | all-to-all | bytes 524288 | tf_op jit(solution)/shard_map/all_to_all | solution.py:115
  247.7 20.9 %all_to_all.112 = f32[2,32,4,4,128]{4,3,2,0,1:T(4,128)S(1)} all-to-all(f32[2,32,4,4,128]{4,3,2,0,1:T(4,128)S(1)} %copy.35), channel_id=1, replica_groups=mesh['tm'=32,'space'=8] {'tm'}, dimensions={1} | all-to-all | bytes 1048576 | tf_op jit(solution)/shard_map/all_to_all | solution.py:116
  268.9 3.0 collective-permute-start.23
  272.0 1.5 collective-permute-start.22
  273.9 5.3 %collective-permute-done.22 = f32[2,1,1,128,128]{4,3,2,1,0:T(8,128)S(1)} collective-permute-done((f32[2,1,1,128,128]{4,3,2,1,0:T(8,128)S(1)}, f32[2,1,1,128,128]{4,3,2,1,0:T(8,128)S(1)}, u32[]{:S(2)}, u32[]{:S(2)}) %collective-permute-start.22) | collective-permute-done | bytes 131104 | tf_op jit(solution)/shard_map/ppermute | solution.py:29
  280.4 2.8 collective-permute-start.25
  285.2 5.3 %collective-permute-done.24 = f32[2,1,1,128,128]{4,3,2,1,0:T(8,128)S(1)} collective-permute-done((f32[2,1,1,128,128]{4,3,2,1,0:T(8,128)S(1)}, f32[2,1,1,128,128]{4,3,2,1,0:T(8,128)S(1)}, u32[]{:S(2)}, u32[]{:S(2)}) %collective-permute-start.24) | collective-permute-done | bytes 131104 | tf_op jit(solution)/shard_map/ppermute | solution.py:29
  291.7 2.8 collective-permute-start.27
  296.5 6.7 %collective-permute-done.26 = f32[2,1,1,128,128]{4,3,2,1,0:T(8,128)S(1)} collective-permute-done((f32[2,1,1,128,128]{4,3,2,1,0:T(8,128)S(1)}, f32[2,1,1,128,128]{4,3,2,1,0:T(8,128)S(1)}, u32[]{:S(2)}, u32[]{:S(2)}) %collective-permute-start.26) | collective-permute-done | bytes 131104 | tf_op jit(solution)/shard_map/ppermute | solution.py:29
  304.4 2.8 collective-permute-start.29
  309.1 6.7 %collective-permute-done.28 = f32[2,1,1,128,128]{4,3,2,1,0:T(8,128)S(1)} collective-permute-done((f32[2,1,1,128,128]{4,3,2,1,0:T(8,128)S(1)}, f32[2,1,1,128,128]{4,3,2,1,0:T(8,128)S(1)}, u32[]{:S(2)}, u32[]{:S(2)}) %collective-permute-start.28) | collective-permute-done | bytes 131104 | tf_op jit(solution)/shard_map/ppermute | solution.py:29
  317.1 2.1 collective-permute-start.31
  321.1 5.3 %collective-permute-done.30 = f32[2,1,1,128,128]{4,3,2,1,0:T(8,128)S(1)} collective-permute-done((f32[2,1,1,128,128]{4,3,2,1,0:T(8,128)S(1)}, f32[2,1,1,128,128]{4,3,2,1,0:T(8,128)S(1)}, u32[]{:S(2)}, u32[]{:S(2)}) %collective-permute-start.30) | collective-permute-done | bytes 131104 | tf_op jit(solution)/shard_map/ppermute | solution.py:29
  327.6 2.8 collective-permute-start.33
  332.4 5.3 %collective-permute-done.32 = f32[2,1,1,128,128]{4,3,2,1,0:T(8,128)S(1)} collective-permute-done((f32[2,1,1,128,128]{4,3,2,1,0:T(8,128)S(1)}, f32[2,1,1,128,128]{4,3,2,1,0:T(8,128)S(1)}, u32[]{:S(2)}, u32[]{:S(2)}) %collective-permute-start.32) | collective-permute-done | bytes 131104 | tf_op jit(solution)/shard_map/ppermute | solution.py:29
  338.9 2.8 collective-permute-start.35
  343.7 5.3 %collective-permute-done.34 = f32[2,1,1,128,128]{4,3,2,1,0:T(8,128)S(1)} collective-permute-done((f32[2,1,1,128,128]{4,3,2,1,0:T(8,128)S(1)}, f32[2,1,1,128,128]{4,3,2,1,0:T(8,128)S(1)}, u32[]{:S(2)}, u32[]{:S(2)}) %collective-permute-start.34) | collective-permute-done | bytes 131104 | tf_op jit(solution)/shard_map/ppermute | solution.py:29
  350.2 2.8 collective-permute-start.37
  355.2 5.6 %collective-permute-done.36 = f32[2,1,1,128,128]{4,3,2,1,0:T(8,128)S(1)} collective-permute-done((f32[2,1,1,128,128]{4,3,2,1,0:T(8,128)S(1)}, f32[2,1,1,128,128]{4,3,2,1,0:T(8,128)S(1)}, u32[]{:S(2)}, u32[]{:S(2)}) %collective-permute-start.36) | collective-permute-done | bytes 131104 | tf_op jit(solution)/shard_map/ppermute | solution.py:29
  362.5 31.4 %all_to_all.113 = f32[2,1,4,128,128]{4,2,1,0,3:T(4,128)S(1)} all-to-all(f32[2,1,4,128,128]{4,2,1,0,3:T(4,128)S(1)} %copy.38), channel_id=1, replica_groups=mesh['tm'=32,'space'=8] {'tm'}, dimensions={3} | all-to-all | bytes 1048576 | tf_op jit(solution)/shard_map/all_to_all | solution.py:126
  395.4 16.6 %all_to_all.114 = f32[32,4,4,128]{3,2,1,0:T(4,128)S(1)} all-to-all(f32[32,4,4,128]{3,2,1,0:T(4,128)S(1)} %reshape.490), channel_id=1, replica_groups=mesh['tm'=32,'space'=8] {'tm'}, dimensions={0} | all-to-all | bytes 524288 | tf_op jit(solution)/shard_map/all_to_all | solution.py:132
  (166 shorter events, 67.0 us)
Async XLA Ops:
  0.0 17.2 %copy-start.1 = (f32[4,128,128]{2,1,0:T(8,128)S(1)}, f32[4,128,128]{2,1,0:T(8,128)}, u32[]{:S(2)}) copy-start(f32[4,128,128]{2,1,0:T(8,128)} %param.5) | copy-start | bytes 786436
  0.0 17.5 %collective-permute-start.2 = (f32[4,128,128]{2,1,0:T(8,128)}, f32[4,128,128]{2,1,0:T(8,128)S(1)}, u32[]{:S(2)}, u32[]{:S(2)}) collective-permute-start(f32[4,128,128]{2,1,0:T(8,128)} %param.5), channel_id=1, source_target_pairs={{0,8},{8,16},{16,24},{24,32},{32,40},{40,48},{48,56},{56,64},{64,7... | collective-permute-start | bytes 786440 | tf_op jit(solution)/shard_map/ppermute | solution.py:18
  5.1 12.5 %copy-start = (f32[4,128,128]{2,1,0:T(8,128)S(1)}, f32[4,128,128]{2,1,0:T(8,128)}, u32[]{:S(2)}) copy-start(f32[4,128,128]{2,1,0:T(8,128)} %param.6) | copy-start | bytes 786436
  5.1 12.5 %copy-start.2 = (f32[1,4,128,128]{3,2,1,0:T(8,128)S(1)}, f32[1,4,128,128]{3,2,1,0:T(8,128)}, u32[]{:S(2)}) copy-start(f32[1,4,128,128]{3,2,1,0:T(8,128)} %param.4) | copy-start | bytes 786436
  6.0 7.3 %collective-permute-start.1 = (f32[1,1,128,128]{3,2,1,0:T(8,128)S(1)}, f32[1,1,128,128]{3,2,1,0:T(8,128)S(1)}, u32[]{:S(2)}, u32[]{:S(2)}) collective-permute-start(f32[1,1,128,128]{3,2,1,0:T(8,128)S(1)} %get-tuple-element.90), channel_id=1, source_target_pairs={{0,1},{1,2},{2,3},{3,4},{4,5},{5,6},{6,7},{8,9},{9,10},{10,11},{11... | collective-permute-start | bytes 196616 | tf_op jit(solution)/shard_map/ppermute | solution.py:26
  10.7 6.6 %collective-permute-start = (f32[1,1,128,128]{3,2,1,0:T(8,128)S(1)}, f32[1,1,128,128]{3,2,1,0:T(8,128)S(1)}, u32[]{:S(2)}, u32[]{:S(2)}) collective-permute-start(f32[1,1,128,128]{3,2,1,0:T(8,128)S(1)} %get-tuple-element.91), channel_id=1, source_target_pairs={{1,0},{2,1},{3,2},{4,3},{5,4},{6,5},{7,6},{9,8},{10,9},{11,10},{12... | collective-permute-start | bytes 196616 | tf_op jit(solution)/shard_map/ppermute | solution.py:29
  41.4 22.1 %all-to-all-start.1 = ((f32[2,32,4,4,128]{4,3,2,0,1:T(4,128)}), f32[2,32,4,4,128]{4,3,2,0,1:T(4,128)S(1)}, u32[]{:S(2)}, u32[]{:S(2)}) async-start(f32[2,32,4,4,128]{4,3,2,0,1:T(4,128)} %copy.25), calls=%async_computation.1 | async-start | bytes 1048576 | tf_op jit(solution)/shard_map/all_to_all | solution.py:116
  63.8 7.5 %collective-permute-start.4 = (f32[2,1,1,128,128]{4,3,2,1,0:T(8,128)S(1)}, f32[2,1,1,128,128]{4,3,2,1,0:T(8,128)S(1)}, u32[]{:S(2)}, u32[]{:S(2)}) collective-permute-start(f32[2,1,1,128,128]{4,3,2,1,0:T(8,128)S(1)} %get-tuple-element.84), channel_id=1, source_target_pairs={{0,1},{1,2},{2,3},{3,4},{4,5},{5,6},{6,7},{8,9},{9,10},{10,11},{11... | collective-permute-start | bytes 393224 | tf_op jit(solution)/shard_map/ppermute | solution.py:26
  69.4 7.2 %collective-permute-start.3 = (f32[2,1,1,128,128]{4,3,2,1,0:T(8,128)S(1)}, f32[2,1,1,128,128]{4,3,2,1,0:T(8,128)S(1)}, u32[]{:S(2)}, u32[]{:S(2)}) collective-permute-start(f32[2,1,1,128,128]{4,3,2,1,0:T(8,128)S(1)} %get-tuple-element.85), channel_id=1, source_target_pairs={{1,0},{2,1},{3,2},{4,3},{5,4},{6,5},{7,6},{9,8},{10,9},{11,10},{12... | collective-permute-start | bytes 393224 | tf_op jit(solution)/shard_map/ppermute | solution.py:29
  77.8 6.1 %collective-permute-start.6 = (f32[2,1,1,128,128]{4,3,2,1,0:T(8,128)S(1)}, f32[2,1,1,128,128]{4,3,2,1,0:T(8,128)S(1)}, u32[]{:S(2)}, u32[]{:S(2)}) collective-permute-start(f32[2,1,1,128,128]{4,3,2,1,0:T(8,128)S(1)} %get-tuple-element.82), channel_id=1, source_target_pairs={{0,1},{1,2},{2,3},{3,4},{4,5},{5,6},{6,7},{8,9},{9,10},{10,11},{11... | collective-permute-start | bytes 393224 | tf_op jit(solution)/shard_map/ppermute | solution.py:26
  82.0 7.8 %collective-permute-start.5 = (f32[2,1,1,128,128]{4,3,2,1,0:T(8,128)S(1)}, f32[2,1,1,128,128]{4,3,2,1,0:T(8,128)S(1)}, u32[]{:S(2)}, u32[]{:S(2)}) collective-permute-start(f32[2,1,1,128,128]{4,3,2,1,0:T(8,128)S(1)} %get-tuple-element.83), channel_id=1, source_target_pairs={{1,0},{2,1},{3,2},{4,3},{5,4},{6,5},{7,6},{9,8},{10,9},{11,10},{12... | collective-permute-start | bytes 393224 | tf_op jit(solution)/shard_map/ppermute | solution.py:29
  91.1 6.7 %collective-permute-start.8 = (f32[2,1,1,128,128]{4,3,2,1,0:T(8,128)S(1)}, f32[2,1,1,128,128]{4,3,2,1,0:T(8,128)S(1)}, u32[]{:S(2)}, u32[]{:S(2)}) collective-permute-start(f32[2,1,1,128,128]{4,3,2,1,0:T(8,128)S(1)} %get-tuple-element.80), channel_id=1, source_target_pairs={{0,1},{1,2},{2,3},{3,4},{4,5},{5,6},{6,7},{8,9},{9,10},{10,11},{11... | collective-permute-start | bytes 393224 | tf_op jit(solution)/shard_map/ppermute | solution.py:26
  95.8 8.6 %collective-permute-start.7 = (f32[2,1,1,128,128]{4,3,2,1,0:T(8,128)S(1)}, f32[2,1,1,128,128]{4,3,2,1,0:T(8,128)S(1)}, u32[]{:S(2)}, u32[]{:S(2)}) collective-permute-start(f32[2,1,1,128,128]{4,3,2,1,0:T(8,128)S(1)} %get-tuple-element.81), channel_id=1, source_target_pairs={{1,0},{2,1},{3,2},{4,3},{5,4},{6,5},{7,6},{9,8},{10,9},{11,10},{12... | collective-permute-start | bytes 393224 | tf_op jit(solution)/shard_map/ppermute | solution.py:29
  105.7 6.6 %collective-permute-start.10 = (f32[2,1,1,128,128]{4,3,2,1,0:T(8,128)S(1)}, f32[2,1,1,128,128]{4,3,2,1,0:T(8,128)S(1)}, u32[]{:S(2)}, u32[]{:S(2)}) collective-permute-start(f32[2,1,1,128,128]{4,3,2,1,0:T(8,128)S(1)} %get-tuple-element.78), channel_id=1, source_target_pairs={{0,1},{1,2},{2,3},{3,4},{4,5},{5,6},{6,7},{8,9},{9,10},{10,11},{11... | collective-permute-start | bytes 393224 | tf_op jit(solution)/shard_map/ppermute | solution.py:26
  110.3 7.9 %collective-permute-start.9 = (f32[2,1,1,128,128]{4,3,2,1,0:T(8,128)S(1)}, f32[2,1,1,128,128]{4,3,2,1,0:T(8,128)S(1)}, u32[]{:S(2)}, u32[]{:S(2)}) collective-permute-start(f32[2,1,1,128,128]{4,3,2,1,0:T(8,128)S(1)} %get-tuple-element.79), channel_id=1, source_target_pairs={{1,0},{2,1},{3,2},{4,3},{5,4},{6,5},{7,6},{9,8},{10,9},{11,10},{12... | collective-permute-start | bytes 393224 | tf_op jit(solution)/shard_map/ppermute | solution.py:29
  119.5 6.6 %collective-permute-start.12 = (f32[2,1,1,128,128]{4,3,2,1,0:T(8,128)S(1)}, f32[2,1,1,128,128]{4,3,2,1,0:T(8,128)S(1)}, u32[]{:S(2)}, u32[]{:S(2)}) collective-permute-start(f32[2,1,1,128,128]{4,3,2,1,0:T(8,128)S(1)} %get-tuple-element.76), channel_id=1, source_target_pairs={{0,1},{1,2},{2,3},{3,4},{4,5},{5,6},{6,7},{8,9},{9,10},{10,11},{11... | collective-permute-start | bytes 393224 | tf_op jit(solution)/shard_map/ppermute | solution.py:26
  124.2 8.6 %collective-permute-start.11 = (f32[2,1,1,128,128]{4,3,2,1,0:T(8,128)S(1)}, f32[2,1,1,128,128]{4,3,2,1,0:T(8,128)S(1)}, u32[]{:S(2)}, u32[]{:S(2)}) collective-permute-start(f32[2,1,1,128,128]{4,3,2,1,0:T(8,128)S(1)} %get-tuple-element.77), channel_id=1, source_target_pairs={{1,0},{2,1},{3,2},{4,3},{5,4},{6,5},{7,6},{9,8},{10,9},{11,10},{12... | collective-permute-start | bytes 393224 | tf_op jit(solution)/shard_map/ppermute | solution.py:29
  134.0 3.4 collective-permute-start.14
  135.5 7.2 %collective-permute-start.13 = (f32[2,1,1,128,128]{4,3,2,1,0:T(8,128)S(1)}, f32[2,1,1,128,128]{4,3,2,1,0:T(8,128)S(1)}, u32[]{:S(2)}, u32[]{:S(2)}) collective-permute-start(f32[2,1,1,128,128]{4,3,2,1,0:T(8,128)S(1)} %get-tuple-element.75), channel_id=1, source_target_pairs={{1,0},{2,1},{3,2},{4,3},{5,4},{6,5},{7,6},{9,8},{10,9},{11,10},{12... | collective-permute-start | bytes 393224 | tf_op jit(solution)/shard_map/ppermute | solution.py:29
  143.9 4.8 %collective-permute-start.16 = (f32[2,1,1,128,128]{4,3,2,1,0:T(8,128)S(1)}, f32[2,1,1,128,128]{4,3,2,1,0:T(8,128)S(1)}, u32[]{:S(2)}, u32[]{:S(2)}) collective-permute-start(f32[2,1,1,128,128]{4,3,2,1,0:T(8,128)S(1)} %get-tuple-element.72), channel_id=1, source_target_pairs={{0,1},{1,2},{2,3},{3,4},{4,5},{5,6},{6,7},{8,9},{9,10},{10,11},{11... | collective-permute-start | bytes 393224 | tf_op jit(solution)/shard_map/ppermute | solution.py:26
  146.8 7.2 %collective-permute-start.15 = (f32[2,1,1,128,128]{4,3,2,1,0:T(8,128)S(1)}, f32[2,1,1,128,128]{4,3,2,1,0:T(8,128)S(1)}, u32[]{:S(2)}, u32[]{:S(2)}) collective-permute-start(f32[2,1,1,128,128]{4,3,2,1,0:T(8,128)S(1)} %get-tuple-element.73), channel_id=1, source_target_pairs={{1,0},{2,1},{3,2},{4,3},{5,4},{6,5},{7,6},{9,8},{10,9},{11,10},{12... | collective-permute-start | bytes 393224 | tf_op jit(solution)/shard_map/ppermute | solution.py:29
  155.2 4.8 %collective-permute-start.18 = (f32[2,1,1,128,128]{4,3,2,1,0:T(8,128)S(1)}, f32[2,1,1,128,128]{4,3,2,1,0:T(8,128)S(1)}, u32[]{:S(2)}, u32[]{:S(2)}) collective-permute-start(f32[2,1,1,128,128]{4,3,2,1,0:T(8,128)S(1)} %get-tuple-element.70), channel_id=1, source_target_pairs={{0,1},{1,2},{2,3},{3,4},{4,5},{5,6},{6,7},{8,9},{9,10},{10,11},{11... | collective-permute-start | bytes 393224 | tf_op jit(solution)/shard_map/ppermute | solution.py:26
  158.1 7.2 %collective-permute-start.17 = (f32[2,1,1,128,128]{4,3,2,1,0:T(8,128)S(1)}, f32[2,1,1,128,128]{4,3,2,1,0:T(8,128)S(1)}, u32[]{:S(2)}, u32[]{:S(2)}) collective-permute-start(f32[2,1,1,128,128]{4,3,2,1,0:T(8,128)S(1)} %get-tuple-element.71), channel_id=1, source_target_pairs={{1,0},{2,1},{3,2},{4,3},{5,4},{6,5},{7,6},{9,8},{10,9},{11,10},{12... | collective-permute-start | bytes 393224 | tf_op jit(solution)/shard_map/ppermute | solution.py:29
  216.0 14.2 %collective-permute-start.21 = (f32[4,128,128]{2,1,0:T(8,128)S(1)}, f32[4,128,128]{2,1,0:T(8,128)S(1)}, u32[]{:S(2)}, u32[]{:S(2)}) collective-permute-start(f32[4,128,128]{2,1,0:T(8,128)S(1)} %add.711), channel_id=1, source_target_pairs={{0,8},{8,16},{16,24},{24,32},{32,40},{40,48},{48,56},{56,64},{64,7... | collective-permute-start | bytes 786440 | tf_op jit(solution)/shard_map/ppermute | solution.py:18
  219.9 6.4 %collective-permute-start.20 = (f32[1,1,128,128]{3,2,1,0:T(8,128)S(1)}, f32[1,1,128,128]{3,2,1,0:T(8,128)S(1)}, u32[]{:S(2)}, u32[]{:S(2)}) collective-permute-start(f32[1,1,128,128]{3,2,1,0:T(8,128)S(1)} %get-tuple-element.88), channel_id=1, source_target_pairs={{0,1},{1,2},{2,3},{3,4},{4,5},{5,6},{6,7},{8,9},{9,10},{10,11},{11... | collective-permute-start | bytes 196616 | tf_op jit(solution)/shard_map/ppermute | solution.py:26
  222.9 7.1 %collective-permute-start.19 = (f32[1,1,128,128]{3,2,1,0:T(8,128)S(1)}, f32[1,1,128,128]{3,2,1,0:T(8,128)S(1)}, u32[]{:S(2)}, u32[]{:S(2)}) collective-permute-start(f32[1,1,128,128]{3,2,1,0:T(8,128)S(1)} %get-tuple-element.89), channel_id=1, source_target_pairs={{1,0},{2,1},{3,2},{4,3},{5,4},{6,5},{7,6},{9,8},{10,9},{11,10},{12... | collective-permute-start | bytes 196616 | tf_op jit(solution)/shard_map/ppermute | solution.py:29
  268.9 4.9 %collective-permute-start.23 = (f32[2,1,1,128,128]{4,3,2,1,0:T(8,128)S(1)}, f32[2,1,1,128,128]{4,3,2,1,0:T(8,128)S(1)}, u32[]{:S(2)}, u32[]{:S(2)}) collective-permute-start(f32[2,1,1,128,128]{4,3,2,1,0:T(8,128)S(1)} %get-tuple-element.64), channel_id=1, source_target_pairs={{0,1},{1,2},{2,3},{3,4},{4,5},{5,6},{6,7},{8,9},{9,10},{10,11},{11... | collective-permute-start | bytes 393224 | tf_op jit(solution)/shard_map/ppermute | solution.py:26
  272.0 7.2 %collective-permute-start.22 = (f32[2,1,1,128,128]{4,3,2,1,0:T(8,128)S(1)}, f32[2,1,1,128,128]{4,3,2,1,0:T(8,128)S(1)}, u32[]{:S(2)}, u32[]{:S(2)}) collective-permute-start(f32[2,1,1,128,128]{4,3,2,1,0:T(8,128)S(1)} %get-tuple-element.65), channel_id=1, source_target_pairs={{1,0},{2,1},{3,2},{4,3},{5,4},{6,5},{7,6},{9,8},{10,9},{11,10},{12... | collective-permute-start | bytes 393224 | tf_op jit(solution)/shard_map/ppermute | solution.py:29
  280.4 4.7 %collective-permute-start.25 = (f32[2,1,1,128,128]{4,3,2,1,0:T(8,128)S(1)}, f32[2,1,1,128,128]{4,3,2,1,0:T(8,128)S(1)}, u32[]{:S(2)}, u32[]{:S(2)}) collective-permute-start(f32[2,1,1,128,128]{4,3,2,1,0:T(8,128)S(1)} %get-tuple-element.62), channel_id=1, source_target_pairs={{0,1},{1,2},{2,3},{3,4},{4,5},{5,6},{6,7},{8,9},{9,10},{10,11},{11... | collective-permute-start | bytes 393224 | tf_op jit(solution)/shard_map/ppermute | solution.py:26
  283.3 7.2 %collective-permute-start.24 = (f32[2,1,1,128,128]{4,3,2,1,0:T(8,128)S(1)}, f32[2,1,1,128,128]{4,3,2,1,0:T(8,128)S(1)}, u32[]{:S(2)}, u32[]{:S(2)}) collective-permute-start(f32[2,1,1,128,128]{4,3,2,1,0:T(8,128)S(1)} %get-tuple-element.63), channel_id=1, source_target_pairs={{1,0},{2,1},{3,2},{4,3},{5,4},{6,5},{7,6},{9,8},{10,9},{11,10},{12... | collective-permute-start | bytes 393224 | tf_op jit(solution)/shard_map/ppermute | solution.py:29
  291.7 4.8 %collective-permute-start.27 = (f32[2,1,1,128,128]{4,3,2,1,0:T(8,128)S(1)}, f32[2,1,1,128,128]{4,3,2,1,0:T(8,128)S(1)}, u32[]{:S(2)}, u32[]{:S(2)}) collective-permute-start(f32[2,1,1,128,128]{4,3,2,1,0:T(8,128)S(1)} %get-tuple-element.60), channel_id=1, source_target_pairs={{0,1},{1,2},{2,3},{3,4},{4,5},{5,6},{6,7},{8,9},{9,10},{10,11},{11... | collective-permute-start | bytes 393224 | tf_op jit(solution)/shard_map/ppermute | solution.py:26
  294.6 8.6 %collective-permute-start.26 = (f32[2,1,1,128,128]{4,3,2,1,0:T(8,128)S(1)}, f32[2,1,1,128,128]{4,3,2,1,0:T(8,128)S(1)}, u32[]{:S(2)}, u32[]{:S(2)}) collective-permute-start(f32[2,1,1,128,128]{4,3,2,1,0:T(8,128)S(1)} %get-tuple-element.61), channel_id=1, source_target_pairs={{1,0},{2,1},{3,2},{4,3},{5,4},{6,5},{7,6},{9,8},{10,9},{11,10},{12... | collective-permute-start | bytes 393224 | tf_op jit(solution)/shard_map/ppermute | solution.py:29
  304.4 4.7 %collective-permute-start.29 = (f32[2,1,1,128,128]{4,3,2,1,0:T(8,128)S(1)}, f32[2,1,1,128,128]{4,3,2,1,0:T(8,128)S(1)}, u32[]{:S(2)}, u32[]{:S(2)}) collective-permute-start(f32[2,1,1,128,128]{4,3,2,1,0:T(8,128)S(1)} %get-tuple-element.58), channel_id=1, source_target_pairs={{0,1},{1,2},{2,3},{3,4},{4,5},{5,6},{6,7},{8,9},{9,10},{10,11},{11... | collective-permute-start | bytes 393224 | tf_op jit(solution)/shard_map/ppermute | solution.py:26
  307.2 8.6 %collective-permute-start.28 = (f32[2,1,1,128,128]{4,3,2,1,0:T(8,128)S(1)}, f32[2,1,1,128,128]{4,3,2,1,0:T(8,128)S(1)}, u32[]{:S(2)}, u32[]{:S(2)}) collective-permute-start(f32[2,1,1,128,128]{4,3,2,1,0:T(8,128)S(1)} %get-tuple-element.59), channel_id=1, source_target_pairs={{1,0},{2,1},{3,2},{4,3},{5,4},{6,5},{7,6},{9,8},{10,9},{11,10},{12... | collective-permute-start | bytes 393224 | tf_op jit(solution)/shard_map/ppermute | solution.py:29
  317.1 4.0 collective-permute-start.31
  319.2 7.2 %collective-permute-start.30 = (f32[2,1,1,128,128]{4,3,2,1,0:T(8,128)S(1)}, f32[2,1,1,128,128]{4,3,2,1,0:T(8,128)S(1)}, u32[]{:S(2)}, u32[]{:S(2)}) collective-permute-start(f32[2,1,1,128,128]{4,3,2,1,0:T(8,128)S(1)} %get-tuple-element.57), channel_id=1, source_target_pairs={{1,0},{2,1},{3,2},{4,3},{5,4},{6,5},{7,6},{9,8},{10,9},{11,10},{12... | collective-permute-start | bytes 393224 | tf_op jit(solution)/shard_map/ppermute | solution.py:29
  327.6 4.7 %collective-permute-start.33 = (f32[2,1,1,128,128]{4,3,2,1,0:T(8,128)S(1)}, f32[2,1,1,128,128]{4,3,2,1,0:T(8,128)S(1)}, u32[]{:S(2)}, u32[]{:S(2)}) collective-permute-start(f32[2,1,1,128,128]{4,3,2,1,0:T(8,128)S(1)} %get-tuple-element.54), channel_id=1, source_target_pairs={{0,1},{1,2},{2,3},{3,4},{4,5},{5,6},{6,7},{8,9},{9,10},{10,11},{11... | collective-permute-start | bytes 393224 | tf_op jit(solution)/shard_map/ppermute | solution.py:26
  330.5 7.2 %collective-permute-start.32 = (f32[2,1,1,128,128]{4,3,2,1,0:T(8,128)S(1)}, f32[2,1,1,128,128]{4,3,2,1,0:T(8,128)S(1)}, u32[]{:S(2)}, u32[]{:S(2)}) collective-permute-start(f32[2,1,1,128,128]{4,3,2,1,0:T(8,128)S(1)} %get-tuple-element.55), channel_id=1, source_target_pairs={{1,0},{2,1},{3,2},{4,3},{5,4},{6,5},{7,6},{9,8},{10,9},{11,10},{12... | collective-permute-start | bytes 393224 | tf_op jit(solution)/shard_map/ppermute | solution.py:29
  338.9 4.7 %collective-permute-start.35 = (f32[2,1,1,128,128]{4,3,2,1,0:T(8,128)S(1)}, f32[2,1,1,128,128]{4,3,2,1,0:T(8,128)S(1)}, u32[]{:S(2)}, u32[]{:S(2)}) collective-permute-start(f32[2,1,1,128,128]{4,3,2,1,0:T(8,128)S(1)} %get-tuple-element.52), channel_id=1, source_target_pairs={{0,1},{1,2},{2,3},{3,4},{4,5},{5,6},{6,7},{8,9},{9,10},{10,11},{11... | collective-permute-start | bytes 393224 | tf_op jit(solution)/shard_map/ppermute | solution.py:26
  341.8 7.2 %collective-permute-start.34 = (f32[2,1,1,128,128]{4,3,2,1,0:T(8,128)S(1)}, f32[2,1,1,128,128]{4,3,2,1,0:T(8,128)S(1)}, u32[]{:S(2)}, u32[]{:S(2)}) collective-permute-start(f32[2,1,1,128,128]{4,3,2,1,0:T(8,128)S(1)} %get-tuple-element.53), channel_id=1, source_target_pairs={{1,0},{2,1},{3,2},{4,3},{5,4},{6,5},{7,6},{9,8},{10,9},{11,10},{12... | collective-permute-start | bytes 393224 | tf_op jit(solution)/shard_map/ppermute | solution.py:29
  350.2 5.0 %collective-permute-start.37 = (f32[2,1,1,128,128]{4,3,2,1,0:T(8,128)S(1)}, f32[2,1,1,128,128]{4,3,2,1,0:T(8,128)S(1)}, u32[]{:S(2)}, u32[]{:S(2)}) collective-permute-start(f32[2,1,1,128,128]{4,3,2,1,0:T(8,128)S(1)} %get-tuple-element.50), channel_id=1, source_target_pairs={{0,1},{1,2},{2,3},{3,4},{4,5},{5,6},{6,7},{8,9},{9,10},{10,11},{11... | collective-permute-start | bytes 393224 | tf_op jit(solution)/shard_map/ppermute | solution.py:26
  353.1 7.8 %collective-permute-start.36 = (f32[2,1,1,128,128]{4,3,2,1,0:T(8,128)S(1)}, f32[2,1,1,128,128]{4,3,2,1,0:T(8,128)S(1)}, u32[]{:S(2)}, u32[]{:S(2)}) collective-permute-start(f32[2,1,1,128,128]{4,3,2,1,0:T(8,128)S(1)} %get-tuple-element.51), channel_id=1, source_target_pairs={{1,0},{2,1},{3,2},{4,3},{5,4},{6,5},{7,6},{9,8},{10,9},{11,10},{12... | collective-permute-start | bytes 393224 | tf_op jit(solution)/shard_map/ppermute | solution.py:29
where the time goes:
time: 414 us; the launch traced here: 413 us
  blocking collectives  152 us (37%)
  waiting for transfers between devices  128 us (31%)
  starting transfers between devices  98.4 us (24%)
  other arithmetic  23.7 us (6%)
  local copies, waits for them, and re-layouts  6.18 us (1%)
    ppermute x18, waiting for transfers between devices, with_halo(): lax.ppermute(lax.slice_in_dim(block, 0, width, axis=dim), axis, backward)  99.4 us
    all_to_all x2, blocking collectives, body(): lax.all_to_all(solved, 'tm', split_axis=3, concat_axis=1, tiled=True)  62.2 us
    ppermute x18, starting transfers between devices, with_halo(): lax.ppermute(lax.slice_in_dim(block, block.shape[dim] - width, None, axis...  60.4 us
    all_to_all x2, blocking collectives, body(): lax.all_to_all(scaled, 'tm', split_axis=2, concat_axis=0, tiled=True)  35.4 us
    all_to_all x2, blocking collectives, body(): lax.all_to_all(inverse_part, 'tm', split_axis=0, concat_axis=2, tiled=True)  33.2 us
    ppermute x18, starting transfers between devices, with_halo(): lax.ppermute(lax.slice_in_dim(block, 0, width, axis=dim), axis, backward)  23.7 us
    all_to_all x1, blocking collectives, body(): lax.all_to_all(spectrum, 'tm', split_axis=1, concat_axis=3, tiled=True)  20.9 us
    all_to_all x1, waiting for transfers between devices, body(): lax.all_to_all(spectrum, 'tm', split_axis=1, concat_axis=3, tiled=True)  16.5 us
  transfers between devices with their start and end apart: 39, of which 36 were waited for; matrix products, arithmetic and copies ran while one was open for 1% of the time, Pallas kernels for 0%

commit v1 on v0

v1 whole, which is shorter than its diff:
```python
import functools
import math

import jax
import jax.numpy as jnp
import numpy as np
from jax import lax
from jax.experimental import pallas as pl
from jax.experimental.pallas import tpu as pltpu
from jax.sharding import PartitionSpec as P

STEPS = 32
ALPHA = 0.1
RHO = ALPHA ** (1.0 / STEPS)
GAMMA = [ALPHA ** (n / STEPS) for n in range(STEPS)]
GROUPS = 2
MESH = pl.DeviceIdType.MESH
F32 = jnp.float32


def real_fft(xs):
    size = len(xs)
    if size == 2:
        return [xs[0] + xs[1], xs[0] - xs[1]], [None, None]
    even_re, even_im = real_fft(xs[0::2])
    odd_re, odd_im = real_fft(xs[1::2])
    half, quarter = size // 2, size // 4
    re, im = [None] * (half + 1), [None] * (half + 1)
    re[0], re[half] = even_re[0] + odd_re[0], even_re[0] - odd_re[0]
    for j in range(1, quarter):
        c, s = math.cos(2 * math.pi * j / size), math.sin(2 * math.pi * j / size)
        t_re = c * odd_re[j] + s * odd_im[j]
        t_im = c * odd_im[j] - s * odd_re[j]
        re[j], im[j] = even_re[j] + t_re, even_im[j] + t_im
        re[half - j], im[half - j] = even_re[j] - t_re, t_im - even_im[j]
    re[quarter], im[quarter] = even_re[quarter], -odd_re[quarter]
    return re, im


def real_ifft(re, im):
    half = len(re) - 1
    size = 2 * half
    if size == 2:
        return [re[0] + re[1], re[0] - re[1]]
    quarter = size // 4
    even_re, even_im = [None] * (quarter + 1), [None] * (quarter + 1)
    odd_re, odd_im = [None] * (quarter + 1), [None] * (quarter + 1)
    even_re[0], odd_re[0] = re[0] + re[half], re[0] - re[half]
    for j in range(1, quarter):
        c, s = math.cos(2 * math.pi * j / size), math.sin(2 * math.pi * j / size)
        even_re[j], even_im[j] = re[j] + re[half - j], im[j] - im[half - j]
        t_re, t_im = re[j] - re[half - j], im[j] + im[half - j]
        odd_re[j], odd_im[j] = c * t_re - s * t_im, c * t_im + s * t_re
    even_re[quarter], odd_re[quarter] = 2.0 * re[quarter], -2.0 * im[quarter]
    even = real_ifft(even_re, even_im)
    odd = real_ifft(odd_re, odd_im)
    return [(even, odd)[n % 2][n // 2] for n in range(size)]


def unit_tables():
    slots = STEPS // 2
    j = np.arange(slots)
    theta = 2 * np.pi * j / STEPS
    n = np.arange(STEPS)
    gamma = np.array(GAMMA)
    angle = 2 * np.pi * ((j[:, None] * n[None, :]) % STEPS) / STEPS
    shift_re = RHO * np.cos(theta)
    shift_re_im = shift_re.copy()
    shift_re_im[0] = -RHO
    shift_im = RHO * np.sin(theta)
    shift_im[0] = 0.0
    const_re = (np.cos(angle) * gamma).sum(1)
    const_im = -(np.sin(angle) * gamma).sum(1)
    const_im[0] = (gamma * (-1.0) ** n).sum()
    last = 2 * np.pi * ((j * (STEPS - 1)) % STEPS) / STEPS
    last_re = 2 * np.cos(last) * RHO / STEPS
    last_im = -2 * np.sin(last) * RHO / STEPS
    last_re[0] = RHO / STEPS
    last_im[0] = -RHO / STEPS
    delta_re = np.ones(slots)
    delta_im = np.zeros(slots)
    delta_im[0] = 1.0
    rows = np.stack(
        [shift_re, shift_re_im, shift_im, const_re, const_im, last_re, last_im, delta_re, delta_im]
    )
    rows = rows.reshape(9, GROUPS, 8).transpose(1, 0, 2)
    return np.ascontiguousarray(np.broadcast_to(rows[..., None], (GROUPS, 9, 8, 128))).astype(np.float32)


def unit_of(j, imaginary):
    if j == STEPS // 2:
        j, imaginary = 0, True
    return (j // 8) * 16 + (8 if imaginary else 0) + j % 8


def device_at(m, zz):
    r, along = lax.rem(m, 4), lax.div(m, 4)
    x = r + lax.rem(along, 2) * (3 - 2 * r)
    return (
        lax.rem(x, 2) * 16 + along * 2 + lax.rem(zz, 2),
        lax.div(zz, 2) * 2 + lax.div(x, 2),
    )


def kernel(
    forcing,
    initial,
    coupling,
    velocity,
    table_in,
    out,
    slab,
    params,
    table,
    packed,
    times,
    spread,
    back,
    gathered,
    pack_params,
    own_params,
    near,
    coef,
    diag,
    d,
    total,
    wrap,
    load_sem,
    out_send,
    out_recv,
    back_send,
    back_recv,
    param_send,
    param_recv,
    near_send,
    near_recv,
    halo_send,
    halo_recv,
):
    me_t, me_s = lax.axis_index("tm"), lax.axis_index("space")
    core, along = lax.rem(me_t, 2), lax.rem(lax.div(me_t, 2), 8)
    row, x_hi = lax.div(me_s, 2), lax.rem(me_s, 2)
    x = 2 * x_hi + lax.div(me_t, 16)
    r = x + lax.rem(along, 2) * (3 - 2 * x)
    m = along * 4 + r
    zz = row * 2 + core
    swap = lax.rem(core + x_hi, 2)
    target = m + swap * (3 - 2 * r)

    loads = [
        pltpu.make_async_copy(forcing, slab, load_sem.at[0]),
        pltpu.make_async_copy(table_in, table, load_sem.at[1]),
    ]
    window = pl.ds(pl.multiple_of(lax.div(target, 2) * 8, 8), 8)
    param_loads = [
        pltpu.make_async_copy(coupling.at[:, window], params.at[0], load_sem.at[2]),
        pltpu.make_async_copy(velocity.at[:, :, window], params.at[pl.ds(1, 3)], load_sem.at[3]),
        pltpu.make_async_copy(initial.at[:, window], params.at[4], load_sem.at[4]),
    ]
    for load in loads + param_loads:
        load.start()

    zeros = jnp.zeros((16, 128), F32)
    for g in range(GROUPS):
        for parity in range(2):
            for i in range(4):
                for z, y in ((0, i + 1), (5, i + 1), (i + 1, 0), (i + 1, 5)):
                    d[g, parity, z, y] = zeros
    for side in range(4):
        near[side, 4] = zeros

    barrier = pltpu.get_barrier_semaphore()

    def greet(i, carry):
        t, b = lax.div(i, 2), lax.rem(i, 2)

        @pl.when(jnp.logical_or(t != me_t, b != x_hi))
        def _():
            pl.semaphore_signal(barrier, inc=1, device_id=(t, row * 2 + b), device_id_type=MESH)

        return carry

    lax.fori_loop(0, 64, greet, 0)
    side_device = [
        device_at(m - 1, zz),
        device_at(m + 1, zz),
        device_at(m, zz - 1),
        device_at(m, zz + 1),
    ]
    has = [m > 0, m < 31, zz > 0, zz < 7]
    far_z = [jnp.logical_and(core == 0, row > 0), jnp.logical_and(core == 1, row < 3)]
    for side in (2, 3):

        @pl.when(far_z[side - 2])
        def _():
            pl.semaphore_signal(barrier, inc=1, device_id=side_device[side], device_id_type=MESH)

    low = lax.broadcasted_iota(jnp.int32, (8, 128), 0) < 4
    loads[0].wait()

    def pack(t, carry):
        rows = pl.ds(pl.multiple_of(t * 8, 8), 8)
        v = [slab[z, rows] for z in range(4)]
        w = [pltpu.roll(a, 4, 0) for a in v]
        packed[2 * t, 0:8] = jnp.where(low, v[0], w[1])
        packed[2 * t, 8:16] = jnp.where(low, v[2], w[3])
        packed[2 * t + 1, 0:8] = jnp.where(low, w[0], v[1])
        packed[2 * t + 1, 8:16] = jnp.where(low, w[2], v[3])
        return carry

    lax.fori_loop(0, 16, pack, 0)
    far_count = jnp.logical_or(far_z[0], far_z[1]).astype(jnp.int32)
    pl.semaphore_wait(barrier, 63 + far_count)

    def out_copy(i):
        return pltpu.make_async_remote_copy(
            src_ref=packed.at[i],
            dst_ref=times.at[me_t],
            send_sem=out_send.at[i],
            recv_sem=out_recv.at[me_t],
            device_id=device_at(i, row * 2 + x_hi),
            device_id_type=MESH,
        )

    def is_self(i):
        return jnp.logical_and(i == m, swap == 0)

    def out_start(k, carry):
        i = lax.rem(m + 1 + k, 32)

        @pl.when(jnp.logical_not(is_self(i)))
        def _():
            out_copy(i).start()

        return carry

    lax.fori_loop(0, 32, out_start, 0)

    @pl.when(swap == 0)
    def _():
        times[me_t] = packed[m]

    for load in param_loads:
        load.wait()
    odd = lax.rem(target, 2) == 1
    for f in range(5):
        v = [params[f, z] for z in range(4)]
        w = [pltpu.roll(a, 4, 0) for a in v]
        v, w = [jnp.where(odd, b, a) for a, b in zip(v, w)], [jnp.where(odd, a, b) for a, b in zip(v, w)]
        pack_params[f, 0:8] = jnp.where(low, v[0], w[1])
        pack_params[f, 8:16] = jnp.where(low, v[2], w[3])
    param_copy = pltpu.make_async_remote_copy(
        src_ref=pack_params,
        dst_ref=own_params,
        send_sem=param_send,
        recv_sem=param_recv,
        device_id=device_at(target, row * 2 + 1 - core),
        device_id_type=MESH,
    )
    @pl.when(swap == 1)
    def _():
        param_copy.start()
        param_copy.wait()

    @pl.when(swap == 0)
    def _():
        own_params[...] = pack_params[...]

    def near_copy(side):
        return pltpu.make_async_remote_copy(
            src_ref=own_params.at[4],
            dst_ref=near.at[side, 4],
            send_sem=near_send.at[side],
            recv_sem=near_recv.at[side],
            device_id=side_device[side],
            device_id_type=MESH,
        )

    opposite = (1, 0, 3, 2)
    for side in range(4):

        @pl.when(has[side])
        def _():
            near_copy(side).start()

    c = own_params[0]
    lane = lax.broadcasted_iota(jnp.int32, (16, 128), 1)
    sub = lax.broadcasted_iota(jnp.int32, (16, 128), 0)
    flow = [c * own_params[1 + k] for k in range(3)]
    coefs = [
        c - flow[0],
        c + flow[0],
        c - flow[1],
        c + flow[1],
        jnp.where(lane == 127, 0.0, c - flow[2]),
        jnp.where(lane == 0, 0.0, c + flow[2]),
    ]
    for p in range(16):
        for k in range(6):
            coef[p, k] = jnp.broadcast_to(coefs[k][p : p + 1], (8, 128))
    loads[1].wait()
    middle = 1.0 + 6.0 * c
    for p in range(16):
        mid = jnp.broadcast_to(middle[p : p + 1], (8, 128))
        for g in range(GROUPS):
            d_re, d_im, s_im = mid - table[g, 0], mid - table[g, 1], table[g, 2]
            inv = 1.0 / (d_re * d_re + s_im * s_im)
            diag[g, p, 0] = d_re * inv
            diag[g, p, 1] = d_im / (d_im * d_im + s_im * s_im)
            diag[g, p, 2] = s_im * inv
    for side in range(4):

        @pl.when(has[side])
        def _():
            near_copy(side).wait_send()

        @pl.when(has[opposite[side]])
        def _():
            near_copy(side).wait_recv()

    own = own_params[4]
    after_y, before_y, after_z, before_z = [near[side, 4] for side in range(4)]
    step = lax.rem(sub, 4)
    summed = coefs[0] * jnp.where(sub < 12, pltpu.roll(own, 12, 0), pltpu.roll(after_z, 12, 0))
    summed += coefs[1] * jnp.where(sub >= 4, pltpu.roll(own, 4, 0), pltpu.roll(before_z, 4, 0))
    summed += coefs[2] * jnp.where(step < 3, pltpu.roll(own, 15, 0), pltpu.roll(after_y, 3, 0))
    summed += coefs[3] * jnp.where(step > 0, pltpu.roll(own, 1, 0), pltpu.roll(before_y, 13, 0))
    summed += coefs[4] * pltpu.roll(own, 127, 1) + coefs[5] * pltpu.roll(own, 1, 1)
    source = summed - 6.0 * c * own

    def out_finish(i, carry):
        @pl.when(jnp.logical_not(is_self(i)))
        def _():
            out_copy(i).wait_send()

        @pl.when(jnp.logical_or(i != me_t, swap == 1))
        def _():
            pltpu.make_async_remote_copy(
                src_ref=packed.at[i],
                dst_ref=times.at[i],
                send_sem=out_send.at[i],
                recv_sem=out_recv.at[i],
                device_id=(me_t, me_s),
                device_id_type=MESH,
            ).wait_recv()

        return carry

    lax.fori_loop(0, 32, out_finish, 0)

    def transform(h, carry):
        rows = pl.ds(pl.multiple_of(h * 8, 8), 8)
        re, im = real_fft([GAMMA[n] * times[n, rows] for n in range(32)])
        for j in range(17):
            spread[pl.ds(h * 256 + unit_of(j, False), 8, stride=32), :] = re[j]
            if im[j] is not None:
                spread[pl.ds(h * 256 + unit_of(j, True), 8, stride=32), :] = im[j]
        return carry

    lax.fori_loop(0, 2, transform, 0)

    def halo_copy(g, parity, side):
        if side < 2:
            src, dst = (1, 5) if side == 0 else (4, 0)
            src_ref = d.at[g, parity, pl.ds(1, 4), src]
            dst_ref = d.at[g, parity, pl.ds(1, 4), dst]
        else:
            src, dst = (1, 5) if side == 2 else (4, 0)
            src_ref = d.at[g, parity, src, pl.ds(1, 4)]
            dst_ref = d.at[g, parity, dst, pl.ds(1, 4)]
        return pltpu.make_async_remote_copy(
            src_ref=src_ref,
            dst_ref=dst_ref,
            send_sem=halo_send.at[g, parity, side],
            recv_sem=halo_recv.at[g, parity, side],
            device_id=side_device[side],
            device_id_type=MESH,
        )

    def halo_start(g, parity):
        for side in range(4):

            @pl.when(has[side])
            def _():
                halo_copy(g, parity, side).start()

    def halo_wait(g, parity):
        for side in range(4):

            @pl.when(has[side])
            def _():
                halo_copy(g, parity, side).wait_send()

            @pl.when(has[opposite[side]])
            def _():
                halo_copy(g, parity, side).wait_recv()

    def divide(g, p, s_re, s_im):
        a_re, a_im, b = diag[g, p, 0], diag[g, p, 1], diag[g, p, 2]
        return a_re * s_re + b * s_im, a_im * s_im - b * s_re

    for g in range(GROUPS):
        for p in range(16):
            z, y = p // 4, p % 4
            base = jnp.broadcast_to(source[p : p + 1], (8, 128))
            first = p * 32 + g * 16
            v_re, v_im = divide(
                g,
                p,
                spread[first : first + 8] + table[g, 3] * base,
                spread[first + 8 : first + 16] + table[g, 4] * base,
            )
            d[g, 0, z + 1, y + 1, 0:8] = v_re
            d[g, 0, z + 1, y + 1, 8:16] = v_im
            total[first : first + 8] = v_re
            total[first + 8 : first + 16] = v_im
        halo_start(g, 0)

    def sweep(g, parity, wrapped, send):
        halo_wait(g, parity)
        for p in range(16):
            z, y = p // 4 + 1, p % 4 + 1
            result = []
            for half in range(2):
                rows = slice(half * 8, half * 8 + 8)
                here = d[g, parity, z, y, rows]
                s = coef[p, 0] * d[g, parity, z + 1, y, rows]
                s += coef[p, 1] * d[g, parity, z - 1, y, rows]
                s += coef[p, 2] * d[g, parity, z, y + 1, rows]
                s += coef[p, 3] * d[g, parity, z, y - 1, rows]
                s += coef[p, 4] * pltpu.roll(here, 127, 1)
                s += coef[p, 5] * pltpu.roll(here, 1, 1)
                if wrapped:
                    s -= table[g, 7 + half] * wrap[p]
                result.append(s)
            v_re, v_im = divide(g, p, *result)
            d[g, 1 - parity, z, y, 0:8] = v_re
            d[g, 1 - parity, z, y, 8:16] = v_im
            first = p * 32 + g * 16
            total[first : first + 8] += v_re
            total[first + 8 : first + 16] += v_im
        if send:
            halo_start(g, 1 - parity)

    def both(k, carry):
        for g in range(GROUPS):
            sweep(g, lax.rem(k + 1, 2), False, True)
        return carry

    lax.fori_loop(1, 9, both, 0)
    for p in range(16):
        s = jnp.zeros((8, 128), F32)
        for g in range(GROUPS):
            first = p * 32 + g * 16
            s += table[g, 5] * total[first : first + 8]
            s += table[g, 6] * total[first + 8 : first + 16]
        wrap[p] = jnp.broadcast_to(jnp.sum(s, axis=0, keepdims=True), (8, 128))
    for g in range(GROUPS):
        sweep(g, 0, True, True)
    lax.fori_loop(10, 17, both, 0)
    for g in range(GROUPS):
        sweep(g, 0, False, False)

    def restore(h, carry):
        rows = pl.ds(pl.multiple_of(h * 8, 8), 8)
        re, im = [None] * 17, [None] * 17
        for j in range(17):
            re[j] = total[pl.ds(h * 256 + unit_of(j, False), 8, stride=32), :]
            if 0 < j < 16:
                im[j] = total[pl.ds(h * 256 + unit_of(j, True), 8, stride=32), :]
        for n, value in enumerate(real_ifft(re, im)):
            back[n, rows] = value * (1.0 / (STEPS * GAMMA[n]))
        return carry

    lax.fori_loop(0, 2, restore, 0)

    def back_copy(i):
        return pltpu.make_async_remote_copy(
            src_ref=back.at[i],
            dst_ref=gathered.at[m],
            send_sem=back_send.at[i],
            recv_sem=back_recv.at[m],
            device_id=(i, row * 2 + core),
            device_id_type=MESH,
        )

    def is_own(i):
        return jnp.logical_and(i == me_t, swap == 0)

    def back_start(k, carry):
        i = lax.rem(me_t + 1 + k, 32)

        @pl.when(jnp.logical_not(is_own(i)))
        def _():
            back_copy(i).start()

        return carry

    lax.fori_loop(0, 32, back_start, 0)

    @pl.when(swap == 0)
    def _():
        gathered[m] = back[me_t]

    def back_finish(i, carry):
        @pl.when(jnp.logical_not(is_own(i)))
        def _():
            back_copy(i).wait_send()

        @pl.when(jnp.logical_not(is_self(i)))
        def _():
            pltpu.make_async_remote_copy(
                src_ref=back.at[i],
                dst_ref=gathered.at[i],
                send_sem=back_send.at[i],
                recv_sem=back_recv.at[i],
                device_id=(me_t, me_s),
                device_id_type=MESH,
            ).wait_recv()

        return carry

    lax.fori_loop(0, 32, back_finish, 0)

    def unpack(t, carry):
        rows = pl.ds(pl.multiple_of(t * 8, 8), 8)
        p = [gathered[2 * t, 0:8], gathered[2 * t, 8:16]]
        q = [gathered[2 * t + 1, 0:8], gathered[2 * t + 1, 8:16]]
        for i in range(2):
            out[2 * i, rows] = jnp.where(low, p[i], pltpu.roll(q[i], 4, 0))
            out[2 * i + 1, rows] = jnp.where(low, pltpu.roll(p[i], 4, 0), q[i])
        return carry

    lax.fori_loop(0, 16, unpack, 0)


def body(forcing, initial, coupling, velocity):
    local = forcing.shape[1:]
    table = jnp.asarray(unit_tables())
    hbm = pl.BlockSpec(memory_space=pl.ANY)
    dma = pltpu.SemaphoreType.DMA
    correction = pl.pallas_call(
        kernel,
        out_shape=jax.ShapeDtypeStruct(local, F32),
        in_specs=[hbm] * 5,
        out_specs=pl.BlockSpec(memory_space=pltpu.VMEM),
        scratch_shapes=[
            pltpu.VMEM(local, F32),
            pltpu.VMEM((5, 4, 8, 128), F32),
            pltpu.VMEM((GROUPS, 9, 8, 128), F32),
            pltpu.VMEM((32, 16, 128), F32),
            pltpu.VMEM((32, 16, 128), F32),
            pltpu.VMEM((512, 128), F32),
            pltpu.VMEM((32, 16, 128), F32),
            pltpu.VMEM((32, 16, 128), F32),
            pltpu.VMEM((5, 16, 128), F32),
            pltpu.VMEM((5, 16, 128), F32),
            pltpu.VMEM((4, 5, 16, 128), F32),
            pltpu.VMEM((16, 6, 8, 128), F32),
            pltpu.VMEM((GROUPS, 16, 3, 8, 128), F32),
            pltpu.VMEM((GROUPS, 2, 6, 6, 16, 128), F32),
            pltpu.VMEM((512, 128), F32),
            pltpu.VMEM((16, 8, 128), F32),
            dma((5,)),
            dma((32,)),
            dma((32,)),
            dma((32,)),
            dma((32,)),
            dma,
            dma,
            dma((4,)),
            dma((4,)),
            dma((GROUPS, 2, 4)),
            dma((GROUPS, 2, 4)),
        ],
        compiler_params=pltpu.CompilerParams(collective_id=0, has_side_effects=True),
    )(forcing[0], initial, coupling, velocity, table)
    return (initial + correction)[None]


def solution(mesh):
    return jax.shard_map(
        body,
        mesh=mesh,
        in_specs=(
            P("tm", "space", None, None),
            P("space", None, None),
            P("space", None, None),
            P(None, "space", None, None),
        ),
        out_specs=P("tm", "space", None, None),
        check_vma=False,
    )
```

time: 414 us -> 98.1 us (0.24)
  blocking collectives: 152 us -> 0 us
  waiting for transfers between devices: 128 us -> 0 us
  starting transfers between devices: 98.4 us -> 0 us
  Pallas kernels: 0 us -> 96.2 us
  other arithmetic: 23.7 us -> 1.68 us
  local copies, waits for them, and re-layouts: 6.18 us -> 0.01 us
    all_to_all x7 -> x0, blocking collectives: 152 us -> none  [the longest x2 62.2 us: body(): lax.all_to_all(solved, 'tm', split_axis=3, concat_axis=1, tiled=True)]
    ppermute x38 -> x0, waiting for transfers between devices: 111 us -> none  [the longest x18 99.4 us: with_halo(): lax.ppermute(lax.slice_in_dim(block, 0, width, axis=dim), axis, backward)]
    pallas_call x0 -> x1, Pallas kernels: none -> 96.2 us  [body(): pl.pallas_call(kernel, out_shape=jax.ShapeDtypeStruct(local, F32), in_spe...]
    ppermute x38 -> x0, starting transfers between devices: 93 us -> none  [the longest x18 60.4 us: with_halo(): lax.ppermute(lax.slice_in_dim(block, block.shape[dim] - width, None, axis...]
    all_to_all x1 -> x0, waiting for transfers between devices: 16.5 us -> none  [body(): lax.all_to_all(spectrum, 'tm', split_axis=1, concat_axis=3, tiled=True)]
    add x18 -> x0, other arithmetic: 9.68 us -> none  [the longest x16 8.91 us: coupled(): total + (coupling - advect[2]) * extended[..., 1:-1, 1:-1, 2:]]
    concatenate x18 -> x0, other arithmetic: 8.58 us -> none  [with_halo(): block = jnp.concatenate([low, block, high], axis=dim)]
    all_to_all x1 -> x0, starting transfers between devices: 5.38 us -> none  [body(): lax.all_to_all(spectrum, 'tm', split_axis=1, concat_axis=3, tiled=True)]
  transfers between devices with their start and end apart: 39 -> 0, of which waited for: 36 -> 0; matrix products, arithmetic and copies ran while one was open for 1% -> 0% of each run, Pallas kernels for 0% -> 0%
where the time goes in v1:
time: 98.1 us; the launch traced here: 97.9 us
  Pallas kernels  96.2 us (98%)
  other arithmetic  1.68 us (2%)
    pallas_call x1, Pallas kernels, body(): pl.pallas_call(kernel, out_shape=jax.ShapeDtypeStruct(local, F32), in_spe...  96.2 us

profile of v1, /device:TPU:1, one launch (start us, length us, event | category | flops | bytes accessed | tf_op | source)
XLA Modules:
  0.0 97.9 jit_solution(2598849158087131246)
XLA Ops:
  0.0 0.0 copy-start
  0.0 96.2 %shard_map.55 = f32[4,128,128]{2,1,0:T(8,128)} custom-call(f32[4,128,128]{2,1,0:T(8,128)} %bitcast.3, f32[4,128,128]{2,1,0:T(8,128)} %initial.1, f32[4,128,128]{2,1,0:T(8,128)} %coupling.1, f32[3,4,128,128]{3,2,1,0:T(8,128)} %velocity.1, f32[2,9,8,128]{3,2,1,0:T(8,128)} %constant.2.clone.table_in), custom_call_target="tpu_custom_call" | custom-call | tf_op jit(solution)/shard_map/pallas_call | solution.py:542
  96.2 0.0 copy-done
  96.2 1.7 %add_bitcast_fusion = f32[1,4,128,128]{3,2,1,0:T(8,128)} fusion(f32[4,128,128]{2,1,0:T(8,128)S(1)} %copy-done, f32[4,128,128]{2,1,0:T(8,128)} %shard_map.55), kind=kLoop, calls=%fused_computation | loop fusion | flops 65536 | bytes 786432 | tf_op jit(solution)/shard_map/broadcast_in_dim | solution.py:578
Async XLA Ops:
  0.0 96.2 %copy-start = (f32[4,128,128]{2,1,0:T(8,128)S(1)}, f32[4,128,128]{2,1,0:T(8,128)}, u32[]{:S(2)}) copy-start(f32[4,128,128]{2,1,0:T(8,128)} %initial.1) | copy-start | bytes 786436

commit v2 on v1

--- a/solution.py
+++ b/solution.py
@@ -13,7 +13,8 @@
 ALPHA = 0.1
 RHO = ALPHA ** (1.0 / STEPS)
 GAMMA = [ALPHA ** (n / STEPS) for n in range(STEPS)]
-GROUPS = 2
+GROUPS = 4
+SLOTS = STEPS // 2 // GROUPS
 MESH = pl.DeviceIdType.MESH
 F32 = jnp.float32
 
@@ -64,33 +65,37 @@
     n = np.arange(STEPS)
     gamma = np.array(GAMMA)
     angle = 2 * np.pi * ((j[:, None] * n[None, :]) % STEPS) / STEPS
-    shift_re = RHO * np.cos(theta)
-    shift_re_im = shift_re.copy()
-    shift_re_im[0] = -RHO
-    shift_im = RHO * np.sin(theta)
-    shift_im[0] = 0.0
-    const_re = (np.cos(angle) * gamma).sum(1)
-    const_im = -(np.sin(angle) * gamma).sum(1)
-    const_im[0] = (gamma * (-1.0) ** n).sum()
     last = 2 * np.pi * ((j * (STEPS - 1)) % STEPS) / STEPS
-    last_re = 2 * np.cos(last) * RHO / STEPS
-    last_im = -2 * np.sin(last) * RHO / STEPS
-    last_re[0] = RHO / STEPS
-    last_im[0] = -RHO / STEPS
-    delta_re = np.ones(slots)
-    delta_im = np.zeros(slots)
-    delta_im[0] = 1.0
-    rows = np.stack(
-        [shift_re, shift_re_im, shift_im, const_re, const_im, last_re, last_im, delta_re, delta_im]
+    re = np.stack(
+        [
+            RHO * np.cos(theta),
+            RHO * np.sin(theta),
+            (np.cos(angle) * gamma).sum(1),
+            2 * np.cos(last) * RHO / STEPS,
+            np.ones(slots),
+        ]
     )
-    rows = rows.reshape(9, GROUPS, 8).transpose(1, 0, 2)
-    return np.ascontiguousarray(np.broadcast_to(rows[..., None], (GROUPS, 9, 8, 128))).astype(np.float32)
+    im = np.stack(
+        [
+            RHO * np.cos(theta),
+            -RHO * np.sin(theta),
+            -(np.sin(angle) * gamma).sum(1),
+            -2 * np.sin(last) * RHO / STEPS,
+            np.zeros(slots),
+        ]
+    )
+    re[1, 0] = im[1, 0] = 0.0
+    re[3, 0] = RHO / STEPS
+    im[:, 0] = [-RHO, 0.0, (gamma * (-1.0) ** n).sum(), -RHO / STEPS, 1.0]
+    rows = np.concatenate([re.reshape(5, GROUPS, SLOTS), im.reshape(5, GROUPS, SLOTS)], axis=2)
+    rows = rows.transpose(1, 0, 2)[..., None]
+    return np.ascontiguousarray(np.broadcast_to(rows, (GROUPS, 5, 8, 128))).astype(np.float32)
 
 
 def unit_of(j, imaginary):
     if j == STEPS // 2:
         j, imaginary = 0, True
-    return (j // 8) * 16 + (8 if imaginary else 0) + j % 8
+    return (j // SLOTS) * 8 + (SLOTS if imaginary else 0) + j % SLOTS
 
 
 def device_at(m, zz):
@@ -123,6 +128,7 @@
     coef,
     diag,
     d,
+    middle_d,
     total,
     wrap,
     load_sem,
@@ -160,40 +166,45 @@
     for load in loads + param_loads:
         load.start()
 
-    zeros = jnp.zeros((16, 128), F32)
+    zeros = jnp.zeros((8, 128), F32)
     for g in range(GROUPS):
         for parity in range(2):
-            for i in range(4):
-                for z, y in ((0, i + 1), (5, i + 1), (i + 1, 0), (i + 1, 5)):
-                    d[g, parity, z, y] = zeros
-    for side in range(4):
-        near[side, 4] = zeros
+            for z in range(8):
+                for y in range(8):
+                    away = max(2 - z, z - 5, 0) + max(2 - y, y - 5, 0)
+                    if 0 < away <= 2:
+                        d[g, parity, z, y] = zeros
+    near[...] = jnp.zeros_like(near)
 
     barrier = pltpu.get_barrier_semaphore()
 
     def greet(i, carry):
-        t, b = lax.div(i, 2), lax.rem(i, 2)
-
-        @pl.when(jnp.logical_or(t != me_t, b != x_hi))
-        def _():
-            pl.semaphore_signal(barrier, inc=1, device_id=(t, row * 2 + b), device_id_type=MESH)
-
-        return carry
-
-    lax.fori_loop(0, 64, greet, 0)
-    side_device = [
-        device_at(m - 1, zz),
-        device_at(m + 1, zz),
-        device_at(m, zz - 1),
-        device_at(m, zz + 1),
-    ]
-    has = [m > 0, m < 31, zz > 0, zz < 7]
-    far_z = [jnp.logical_and(core == 0, row > 0), jnp.logical_and(core == 1, row < 3)]
-    for side in (2, 3):
-
-        @pl.when(far_z[side - 2])
+        t = lax.rem(me_t + 8 + i, 32)
+
+        @pl.when(jnp.logical_or(t != me_t, swap == 1))
+        def _():
+            pl.semaphore_signal(barrier, inc=1, device_id=(t, row * 2 + core), device_id_type=MESH)
+
+        return carry
+
+    sides = [(-1, 0), (1, 0), (0, -1), (0, 1), (-1, -1), (1, 1), (-1, 1), (1, -1)]
+    opposite = [1, 0, 3, 2, 5, 4, 7, 6]
+    in_y = {-1: m > 0, 1: m < 31}
+    in_z = {-1: zz > 0, 1: zz < 7}
+    side_device, has = [], []
+    for by, bz in sides:
+        side_device.append(device_at(m + by, zz + bz))
+        inside = in_y[by] if by else in_z[bz]
+        has.append(jnp.logical_and(in_y[by], in_z[bz]) if by and bz else inside)
+    count = 31 + swap
+    for side in range(8):
+
+        @pl.when(has[side])
         def _():
             pl.semaphore_signal(barrier, inc=1, device_id=side_device[side], device_id_type=MESH)
+
+        count += has[side].astype(jnp.int32)
+    lax.fori_loop(0, 32, greet, 0)
 
     low = lax.broadcasted_iota(jnp.int32, (8, 128), 0) < 4
     loads[0].wait()
@@ -209,8 +220,7 @@
         return carry
 
     lax.fori_loop(0, 16, pack, 0)
-    far_count = jnp.logical_or(far_z[0], far_z[1]).astype(jnp.int32)
-    pl.semaphore_wait(barrier, 63 + far_count)
+    pl.semaphore_wait(barrier, count)
 
     def out_copy(i):
         return pltpu.make_async_remote_copy(
@@ -268,46 +278,50 @@
 
     def near_copy(side):
         return pltpu.make_async_remote_copy(
-            src_ref=own_params.at[4],
-            dst_ref=near.at[side, 4],
+            src_ref=own_params,
+            dst_ref=near.at[side],
             send_sem=near_send.at[side],
             recv_sem=near_recv.at[side],
             device_id=side_device[side],
             device_id_type=MESH,
         )
 
-    opposite = (1, 0, 3, 2)
     for side in range(4):
 
         @pl.when(has[side])
         def _():
             near_copy(side).start()
 
-    c = own_params[0]
     lane = lax.broadcasted_iota(jnp.int32, (16, 128), 1)
     sub = lax.broadcasted_iota(jnp.int32, (16, 128), 0)
-    flow = [c * own_params[1 + k] for k in range(3)]
-    coefs = [
-        c - flow[0],
-        c + flow[0],
-        c - flow[1],
-        c + flow[1],
-        jnp.where(lane == 127, 0.0, c - flow[2]),
-        jnp.where(lane == 0, 0.0, c + flow[2]),
-    ]
-    for p in range(16):
-        for k in range(6):
-            coef[p, k] = jnp.broadcast_to(coefs[k][p : p + 1], (8, 128))
     loads[1].wait()
-    middle = 1.0 + 6.0 * c
-    for p in range(16):
-        mid = jnp.broadcast_to(middle[p : p + 1], (8, 128))
-        for g in range(GROUPS):
-            d_re, d_im, s_im = mid - table[g, 0], mid - table[g, 1], table[g, 2]
-            inv = 1.0 / (d_re * d_re + s_im * s_im)
-            diag[g, p, 0] = d_re * inv
-            diag[g, p, 1] = d_im / (d_im * d_im + s_im * s_im)
-            diag[g, p, 2] = s_im * inv
+
+    def coefficients(ref):
+        c = ref[0]
+        flow = [c * ref[1 + k] for k in range(3)]
+        return c, [
+            c - flow[0],
+            c + flow[0],
+            c - flow[1],
+            c + flow[1],
+            jnp.where(lane == 127, 0.0, c - flow[2]),
+            jnp.where(lane == 0, 0.0, c + flow[2]),
+        ]
+
+    def spread_coefficients(c, coefs, cells):
+        middle = 1.0 + 6.0 * c
+        for p, at in cells:
+            for k in range(6):
+                coef[at, k] = jnp.broadcast_to(coefs[k][p : p + 1], (8, 128))
+            mid = jnp.broadcast_to(middle[p : p + 1], (8, 128))
+            for g in range(GROUPS):
+                d_re, d_im = mid - table[g, 0], table[g, 1]
+                inv = 1.0 / (d_re * d_re + d_im * d_im)
+                diag[g, at, 0] = d_re * inv
+                diag[g, at, 1] = d_im * inv
+
+    c, coefs = coefficients(own_params)
+    spread_coefficients(c, coefs, [(p, p) for p in range(16)])
     for side in range(4):
 
         @pl.when(has[side])
@@ -318,6 +332,10 @@
         def _():
             near_copy(side).wait_recv()
 
+    ring_rows = [[4 * i for i in range(4)], [4 * i + 3 for i in range(4)], range(4), range(12, 16)]
+    for side in range(4):
+        cells = [(p, 16 + side * 4 + i) for i, p in enumerate(ring_rows[side])]
+        spread_coefficients(*coefficients(near.at[side]), cells)
     own = own_params[4]
     after_y, before_y, after_z, before_z = [near[side, 4] for side in range(4)]
     step = lax.rem(sub, 4)
@@ -360,17 +378,20 @@
     lax.fori_loop(0, 2, transform, 0)
 
     def halo_copy(g, parity, side):
-        if side < 2:
-            src, dst = (1, 5) if side == 0 else (4, 0)
-            src_ref = d.at[g, parity, pl.ds(1, 4), src]
-            dst_ref = d.at[g, parity, pl.ds(1, 4), dst]
-        else:
-            src, dst = (1, 5) if side == 2 else (4, 0)
-            src_ref = d.at[g, parity, src, pl.ds(1, 4)]
-            dst_ref = d.at[g, parity, dst, pl.ds(1, 4)]
+        refs = []
+        for shift in (0, 4):
+            at = []
+            for by, bz in ((sides[side][1], sides[side][0]), (sides[side][0], sides[side][1])):
+                if by == 0:
+                    at.append(pl.ds(2, 4))
+                elif bz == 0:
+                    at.append(pl.ds((2 if by < 0 else 4) - by * shift, 2))
+                else:
+                    at.append((2 if by < 0 else 5) - by * shift)
+            refs.append(d.at[g, parity, at[0], at[1]])
         return pltpu.make_async_remote_copy(
-            src_ref=src_ref,
-            dst_ref=dst_ref,
+            src_ref=refs[0],
+            dst_ref=refs[1],
             send_sem=halo_send.at[g, parity, side],
             recv_sem=halo_recv.at[g, parity, side],
             device_id=side_device[side],
@@ -378,88 +399,87 @@
         )
 
     def halo_start(g, parity):
-        for side in range(4):
+        for side in range(8):
 
             @pl.when(has[side])
             def _():
                 halo_copy(g, parity, side).start()
 
     def halo_wait(g, parity):
-        for side in range(4):
+        for side in range(8):
 
             @pl.when(has[side])
             def _():
                 halo_copy(g, parity, side).wait_send()
-
-            @pl.when(has[opposite[side]])
-            def _():
-                halo_copy(g, parity, side).wait_recv()
-
-    def divide(g, p, s_re, s_im):
-        a_re, a_im, b = diag[g, p, 0], diag[g, p, 1], diag[g, p, 2]
-        return a_re * s_re + b * s_im, a_im * s_im - b * s_re
+                halo_copy(g, parity, opposite[side]).wait_recv()
+
+    def divide(g, at, s):
+        return diag[g, at, 0] * s + diag[g, at, 1] * pltpu.roll(s, 4, 0)
+
+    def stencil(field, z, y, at):
+        here = field[z, y]
+        s = coef[at, 0] * field[z + 1, y]
+        s += coef[at, 1] * field[z - 1, y]
+        s += coef[at, 2] * field[z, y + 1]
+        s += coef[at, 3] * field[z, y - 1]
+        s += coef[at, 4] * pltpu.roll(here, 127, 1)
+        s += coef[at, 5] * pltpu.roll(here, 1, 1)
+        return s
 
     for g in range(GROUPS):
         for p in range(16):
             z, y = p // 4, p % 4
             base = jnp.broadcast_to(source[p : p + 1], (8, 128))
-            first = p * 32 + g * 16
-            v_re, v_im = divide(
-                g,
-                p,
-                spread[first : first + 8] + table[g, 3] * base,
-                spread[first + 8 : first + 16] + table[g, 4] * base,
-            )
-            d[g, 0, z + 1, y + 1, 0:8] = v_re
-            d[g, 0, z + 1, y + 1, 8:16] = v_im
-            total[first : first + 8] = v_re
-            total[first + 8 : first + 16] = v_im
+            rows = pl.ds(p * 32 + g * 8, 8)
+            v = divide(g, p, spread[rows] + table[g, 2] * base)
+            d[g, 0, z + 2, y + 2] = v
+            total[rows] = v
         halo_start(g, 0)
 
-    def sweep(g, parity, wrapped, send):
+    ring = [(i, -1) for i in range(4)] + [(i, 4) for i in range(4)]
+    ring = ring + [(-1, i) for i in range(4)] + [(4, i) for i in range(4)]
+    ring = ring[4:8] + ring[0:4] + ring[12:16] + ring[8:12]
+
+    def two_sweeps(g, parity, send):
         halo_wait(g, parity)
-        for p in range(16):
-            z, y = p // 4 + 1, p % 4 + 1
-            result = []
-            for half in range(2):
-                rows = slice(half * 8, half * 8 + 8)
-                here = d[g, parity, z, y, rows]
-                s = coef[p, 0] * d[g, parity, z + 1, y, rows]
-                s += coef[p, 1] * d[g, parity, z - 1, y, rows]
-                s += coef[p, 2] * d[g, parity, z, y + 1, rows]
-                s += coef[p, 3] * d[g, parity, z, y - 1, rows]
-                s += coef[p, 4] * pltpu.roll(here, 127, 1)
-                s += coef[p, 5] * pltpu.roll(here, 1, 1)
-                if wrapped:
-                    s -= table[g, 7 + half] * wrap[p]
-                result.append(s)
-            v_re, v_im = divide(g, p, *result)
-            d[g, 1 - parity, z, y, 0:8] = v_re
-            d[g, 1 - parity, z, y, 8:16] = v_im
-            first = p * 32 + g * 16
-            total[first : first + 8] += v_re
-            total[first + 8 : first + 16] += v_im
+        old, new = d.at[g, parity], d.at[g, 1 - parity]
+        for at in range(32):
+            z, y = (at // 4, at % 4) if at < 16 else ring[at - 16]
+            v = divide(g, at, stencil(old, z + 2, y + 2, at))
+            middle_d[z + 1, y + 1] = v
+            if at < 16:
+                total[pl.ds(at * 32 + g * 8, 8)] += v
+        for at in range(16):
+            z, y = at // 4, at % 4
+            v = divide(g, at, stencil(middle_d, z + 1, y + 1, at))
+            new[z + 2, y + 2] = v
+            total[pl.ds(at * 32 + g * 8, 8)] += v
         if send:
             halo_start(g, 1 - parity)
 
-    def both(k, carry):
+    def all_groups(k, carry):
         for g in range(GROUPS):
-            sweep(g, lax.rem(k + 1, 2), False, True)
-        return carry
-
-    lax.fori_loop(1, 9, both, 0)
+            two_sweeps(g, lax.rem(k, 2), True)
+        return carry
+
+    lax.fori_loop(0, 4, all_groups, 0)
     for p in range(16):
         s = jnp.zeros((8, 128), F32)
         for g in range(GROUPS):
-            first = p * 32 + g * 16
-            s += table[g, 5] * total[first : first + 8]
-            s += table[g, 6] * total[first + 8 : first + 16]
+            s += table[g, 3] * total[pl.ds(p * 32 + g * 8, 8)]
         wrap[p] = jnp.broadcast_to(jnp.sum(s, axis=0, keepdims=True), (8, 128))
     for g in range(GROUPS):
-        sweep(g, 0, True, True)
-    lax.fori_loop(10, 17, both, 0)
+        halo_wait(g, 0)
+        for at in range(16):
+            z, y = at // 4, at % 4
+            s = stencil(d.at[g, 0], z + 2, y + 2, at) - table[g, 4] * wrap[at]
+            v = divide(g, at, s)
+            d[g, 1, z + 2, y + 2] = v
+            total[pl.ds(at * 32 + g * 8, 8)] += v
+        halo_start(g, 1)
+    lax.fori_loop(5, 8, all_groups, 0)
     for g in range(GROUPS):
-        sweep(g, 0, False, False)
+        two_sweeps(g, 0, False)
 
     def restore(h, carry):
         rows = pl.ds(pl.multiple_of(h * 8, 8), 8)
@@ -547,7 +567,7 @@
         scratch_shapes=[
             pltpu.VMEM(local, F32),
             pltpu.VMEM((5, 4, 8, 128), F32),
-            pltpu.VMEM((GROUPS, 9, 8, 128), F32),
+            pltpu.VMEM((GROUPS, 5, 8, 128), F32),
             pltpu.VMEM((32, 16, 128), F32),
             pltpu.VMEM((32, 16, 128), F32),
             pltpu.VMEM((512, 128), F32),
@@ -556,9 +576,10 @@
             pltpu.VMEM((5, 16, 128), F32),
             pltpu.VMEM((5, 16, 128), F32),
             pltpu.VMEM((4, 5, 16, 128), F32),
-            pltpu.VMEM((16, 6, 8, 128), F32),
-            pltpu.VMEM((GROUPS, 16, 3, 8, 128), F32),
-            pltpu.VMEM((GROUPS, 2, 6, 6, 16, 128), F32),
+            pltpu.VMEM((32, 6, 8, 128), F32),
+            pltpu.VMEM((GROUPS, 32, 2, 8, 128), F32),
+            pltpu.VMEM((GROUPS, 2, 8, 8, 8, 128), F32),
+            pltpu.VMEM((6, 6, 8, 128), F32),
             pltpu.VMEM((512, 128), F32),
             pltpu.VMEM((16, 8, 128), F32),
             dma((5,)),
@@ -570,8 +591,8 @@
             dma,
             dma((4,)),
             dma((4,)),
-            dma((GROUPS, 2, 4)),
-            dma((GROUPS, 2, 4)),
+            dma((GROUPS, 2, 8)),
+            dma((GROUPS, 2, 8)),
         ],
         compiler_params=pltpu.CompilerParams(collective_id=0, has_side_effects=True),
     )(forcing[0], initial, coupling, velocity, table)

time: 98.1 us -> 76.1 us (0.78)
  Pallas kernels: 96.2 us -> 73.6 us
    pallas_call x1, Pallas kernels: 96.2 us -> 73.6 us  [body(): pl.pallas_call(kernel, out_shape=jax.ShapeDtypeStruct(local, F32), in_spe...]
where the time goes in v2:
time: 76.1 us; the launch traced here: 75.3 us
  Pallas kernels  73.6 us (97%)
  other arithmetic  1.68 us (2%)
    pallas_call x1, Pallas kernels, body(): pl.pallas_call(kernel, out_shape=jax.ShapeDtypeStruct(local, F32), in_spe...  73.6 us
    broadcast_in_dim x1, other arithmetic, body(): return (initial + correction)[None]  1.68 us

profile of v2, /device:TPU:1, one launch (start us, length us, event | category | flops | bytes accessed | tf_op | source)
XLA Modules:
  0.0 75.3 jit_solution(336457610424601903)
XLA Ops:
  0.0 0.0 copy-start
  0.0 73.6 %shard_map.55 = f32[4,128,128]{2,1,0:T(8,128)} custom-call(f32[4,128,128]{2,1,0:T(8,128)} %bitcast.3, f32[4,128,128]{2,1,0:T(8,128)} %initial.1, f32[4,128,128]{2,1,0:T(8,128)} %coupling.1, f32[3,4,128,128]{3,2,1,0:T(8,128)} %velocity.1, f32[4,5,8,128]{3,2,1,0:T(8,128)} %constant.2.clone.table_in), custom_call_target="tpu_custom_call" | custom-call | tf_op jit(solution)/shard_map/pallas_call | solution.py:562
  73.7 0.0 copy-done
  73.7 1.7 %add_bitcast_fusion = f32[1,4,128,128]{3,2,1,0:T(8,128)} fusion(f32[4,128,128]{2,1,0:T(8,128)S(1)} %copy-done, f32[4,128,128]{2,1,0:T(8,128)} %shard_map.55), kind=kLoop, calls=%fused_computation | loop fusion | flops 65536 | bytes 786432 | tf_op jit(solution)/shard_map/broadcast_in_dim | solution.py:599
Async XLA Ops:
  0.0 73.7 %copy-start = (f32[4,128,128]{2,1,0:T(8,128)S(1)}, f32[4,128,128]{2,1,0:T(8,128)}, u32[]{:S(2)}) copy-start(f32[4,128,128]{2,1,0:T(8,128)} %initial.1) | copy-start | bytes 786436

commit v3 on v2

--- a/solution.py
+++ b/solution.py
@@ -152,6 +152,16 @@
     zz = row * 2 + core
     swap = lax.rem(core + x_hi, 2)
     target = m + swap * (3 - 2 * r)
+    x_lo = x - 2 * x_hi
+
+    far_first = (4, 3, 5, 2, 6, 1, 7, 0)
+    zs, turned = [None] * 8, [None] * 8
+    odd_z = lax.rem(along, 2)
+    for step in range(8):
+        zs[step] = along + step - 8 * (along + step >= 8).astype(jnp.int32)
+        turned[step] = 1 - odd_z if step % 2 else odd_z
+    xs = [x + step - 4 * (x + step >= 4).astype(jnp.int32) for step in range(4)]
+    x_his = [(v >= 2).astype(jnp.int32) for v in xs]
 
     loads = [
         pltpu.make_async_copy(forcing, slab, load_sem.at[0]),
@@ -166,26 +176,7 @@
     for load in loads + param_loads:
         load.start()
 
-    zeros = jnp.zeros((8, 128), F32)
-    for g in range(GROUPS):
-        for parity in range(2):
-            for z in range(8):
-                for y in range(8):
-                    away = max(2 - z, z - 5, 0) + max(2 - y, y - 5, 0)
-                    if 0 < away <= 2:
-                        d[g, parity, z, y] = zeros
-    near[...] = jnp.zeros_like(near)
-
     barrier = pltpu.get_barrier_semaphore()
-
-    def greet(i, carry):
-        t = lax.rem(me_t + 8 + i, 32)
-
-        @pl.when(jnp.logical_or(t != me_t, swap == 1))
-        def _():
-            pl.semaphore_signal(barrier, inc=1, device_id=(t, row * 2 + core), device_id_type=MESH)
-
-        return carry
 
     sides = [(-1, 0), (1, 0), (0, -1), (0, 1), (-1, -1), (1, 1), (-1, 1), (1, -1)]
     opposite = [1, 0, 3, 2, 5, 4, 7, 6]
@@ -196,7 +187,36 @@
         side_device.append(device_at(m + by, zz + bz))
         inside = in_y[by] if by else in_z[bz]
         has.append(jnp.logical_and(in_y[by], in_z[bz]) if by and bz else inside)
+    interior = jnp.logical_and(jnp.logical_and(has[0], has[1]), jnp.logical_and(has[2], has[3]))
+
+    @pl.when(jnp.logical_not(interior))
+    def _():
+        zeros = jnp.zeros((8, 128), F32)
+        for g in range(GROUPS):
+            for parity in range(2):
+                for z in range(8):
+                    for y in range(8):
+                        away = max(2 - z, z - 5, 0) + max(2 - y, y - 5, 0)
+                        if 0 < away <= 2:
+                            d[g, parity, z, y] = zeros
+        near[...] = jnp.zeros_like(near)
+
     count = 31 + swap
+    def senders():
+        for step in far_first:
+            for flip_x in range(2):
+                for flip_core in range(2):
+                    to_x = 1 - x_lo if flip_x else x_lo
+                    to_core = 1 - core if flip_core else core
+                    t = to_x * 16 + zs[step] * 2 + to_core
+                    yield t, step == 0 and flip_x == 0 and flip_core == 0
+
+    for t, mine in senders():
+
+        @pl.when(swap == 1 if mine else True)
+        def _():
+            pl.semaphore_signal(barrier, inc=1, device_id=(t, row * 2 + core), device_id_type=MESH)
+
     for side in range(8):
 
         @pl.when(has[side])
@@ -204,7 +224,6 @@
             pl.semaphore_signal(barrier, inc=1, device_id=side_device[side], device_id_type=MESH)
 
         count += has[side].astype(jnp.int32)
-    lax.fori_loop(0, 32, greet, 0)
 
     low = lax.broadcasted_iota(jnp.int32, (8, 128), 0) < 4
     loads[0].wait()
@@ -222,33 +241,43 @@
     lax.fori_loop(0, 16, pack, 0)
     pl.semaphore_wait(barrier, count)
 
-    def out_copy(i):
-        return pltpu.make_async_remote_copy(
-            src_ref=packed.at[i],
-            dst_ref=times.at[me_t],
-            send_sem=out_send.at[i],
-            recv_sem=out_recv.at[me_t],
-            device_id=device_at(i, row * 2 + x_hi),
-            device_id_type=MESH,
-        )
-
-    def is_self(i):
-        return jnp.logical_and(i == m, swap == 0)
-
-    def out_start(k, carry):
-        i = lax.rem(m + 1 + k, 32)
-
-        @pl.when(jnp.logical_not(is_self(i)))
-        def _():
-            out_copy(i).start()
-
-        return carry
-
-    lax.fori_loop(0, 32, out_start, 0)
+    for step in far_first:
+        for to_x in range(4):
+            chunk = 4 * zs[step] + xs[to_x] + turned[step] * (3 - 2 * xs[to_x])
+            to = (
+                (xs[to_x] - 2 * x_his[to_x]) * 16 + zs[step] * 2 + x_hi,
+                row * 2 + x_his[to_x],
+            )
+
+            @pl.when(swap == 1 if step == 0 and to_x == 0 else True)
+            def _():
+                pltpu.make_async_remote_copy(
+                    src_ref=packed.at[chunk],
+                    dst_ref=times.at[me_t],
+                    send_sem=out_send,
+                    recv_sem=out_recv,
+                    device_id=to,
+                    device_id_type=MESH,
+                ).start()
 
     @pl.when(swap == 0)
     def _():
         times[me_t] = packed[m]
+
+    def finish(src, dst, send_sem, recv_sem):
+        for copies in range(2):
+
+            @pl.when(swap == copies)
+            def _():
+                some = pl.ds(0, 31 + copies)
+                pltpu.make_async_remote_copy(
+                    src_ref=src.at[some],
+                    dst_ref=dst.at[some],
+                    send_sem=send_sem,
+                    recv_sem=recv_sem,
+                    device_id=(me_t, me_s),
+                    device_id_type=MESH,
+                ).wait()
 
     for load in param_loads:
         load.wait()
@@ -346,25 +375,7 @@
     summed += coefs[4] * pltpu.roll(own, 127, 1) + coefs[5] * pltpu.roll(own, 1, 1)
     source = summed - 6.0 * c * own
 
-    def out_finish(i, carry):
-        @pl.when(jnp.logical_not(is_self(i)))
-        def _():
-            out_copy(i).wait_send()
-
-        @pl.when(jnp.logical_or(i != me_t, swap == 1))
-        def _():
-            pltpu.make_async_remote_copy(
-                src_ref=packed.at[i],
-                dst_ref=times.at[i],
-                send_sem=out_send.at[i],
-                recv_sem=out_recv.at[i],
-                device_id=(me_t, me_s),
-                device_id_type=MESH,
-            ).wait_recv()
-
-        return carry
-
-    lax.fori_loop(0, 32, out_finish, 0)
+    finish(packed, times, out_send, out_recv)
 
     def transform(h, carry):
         rows = pl.ds(pl.multiple_of(h * 8, 8), 8)
@@ -392,26 +403,46 @@
         return pltpu.make_async_remote_copy(
             src_ref=refs[0],
             dst_ref=refs[1],
-            send_sem=halo_send.at[g, parity, side],
-            recv_sem=halo_recv.at[g, parity, side],
+            send_sem=halo_send.at[g, parity],
+            recv_sem=halo_recv.at[g, parity],
             device_id=side_device[side],
             device_id_type=MESH,
         )
 
     def halo_start(g, parity):
-        for side in range(8):
-
-            @pl.when(has[side])
+        @pl.when(interior)
+        def _():
+            for side in range(8):
+                halo_copy(g, parity, side).start()
+
+        @pl.when(jnp.logical_not(interior))
+        def _():
+            for side in range(8):
+
+                @pl.when(has[side])
+                def _():
+                    halo_copy(g, parity, side).start()
+
+    whole_y, whole_z = jnp.logical_and(has[0], has[1]), jnp.logical_and(has[2], has[3])
+
+    def halo_wait(g, parity):
+        for tiles, when in (
+            (36, interior),
+            (26, whole_y != whole_z),
+            (17, jnp.logical_not(jnp.logical_or(whole_y, whole_z))),
+        ):
+
+            @pl.when(when)
             def _():
-                halo_copy(g, parity, side).start()
-
-    def halo_wait(g, parity):
-        for side in range(8):
-
-            @pl.when(has[side])
-            def _():
-                halo_copy(g, parity, side).wait_send()
-                halo_copy(g, parity, opposite[side]).wait_recv()
+                amount = spread.at[pl.ds(0, tiles * 8)]
+                pltpu.make_async_remote_copy(
+                    src_ref=amount,
+                    dst_ref=amount,
+                    send_sem=halo_send.at[g, parity],
+                    recv_sem=halo_recv.at[g, parity],
+                    device_id=(me_t, me_s),
+                    device_id_type=MESH,
+                ).wait()
 
     def divide(g, at, s):
         return diag[g, at, 0] * s + diag[g, at, 1] * pltpu.roll(s, 4, 0)
@@ -494,53 +525,24 @@
 
     lax.fori_loop(0, 2, restore, 0)
 
-    def back_copy(i):
-        return pltpu.make_async_remote_copy(
-            src_ref=back.at[i],
-            dst_ref=gathered.at[m],
-            send_sem=back_send.at[i],
-            recv_sem=back_recv.at[m],
-            device_id=(i, row * 2 + core),
-            device_id_type=MESH,
-        )
-
-    def is_own(i):
-        return jnp.logical_and(i == me_t, swap == 0)
-
-    def back_start(k, carry):
-        i = lax.rem(me_t + 1 + k, 32)
-
-        @pl.when(jnp.logical_not(is_own(i)))
-        def _():
-            back_copy(i).start()
-
-        return carry
-
-    lax.fori_loop(0, 32, back_start, 0)
+    for t, mine in senders():
+
+        @pl.when(swap == 1 if mine else True)
+        def _():
+            pltpu.make_async_remote_copy(
+                src_ref=back.at[t],
+                dst_ref=gathered.at[m],
+                send_sem=back_send,
+                recv_sem=back_recv,
+                device_id=(t, row * 2 + core),
+                device_id_type=MESH,
+            ).start()
 
     @pl.when(swap == 0)
     def _():
         gathered[m] = back[me_t]
 
-    def back_finish(i, carry):
-        @pl.when(jnp.logical_not(is_own(i)))
-        def _():
-            back_copy(i).wait_send()
-
-        @pl.when(jnp.logical_not(is_self(i)))
-        def _():
-            pltpu.make_async_remote_copy(
-                src_ref=back.at[i],
-                dst_ref=gathered.at[i],
-                send_sem=back_send.at[i],
-                recv_sem=back_recv.at[i],
-                device_id=(me_t, me_s),
-                device_id_type=MESH,
-            ).wait_recv()
-
-        return carry
-
-    lax.fori_loop(0, 32, back_finish, 0)
+    finish(back, gathered, back_send, back_recv)
 
     def unpack(t, carry):
         rows = pl.ds(pl.multiple_of(t * 8, 8), 8)
@@ -583,16 +585,16 @@
             pltpu.VMEM((512, 128), F32),
             pltpu.VMEM((16, 8, 128), F32),
             dma((5,)),
-            dma((32,)),
-            dma((32,)),
-            dma((32,)),
-            dma((32,)),
+            dma,
+            dma,
+            dma,
+            dma,
             dma,
             dma,
             dma((4,)),
             dma((4,)),
-            dma((GROUPS, 2, 8)),
-            dma((GROUPS, 2, 8)),
+            dma((GROUPS, 2)),
+            dma((GROUPS, 2)),
         ],
         compiler_params=pltpu.CompilerParams(collective_id=0, has_side_effects=True),
     )(forcing[0], initial, coupling, velocity, table)

time: 76.1 us -> 71 us (0.933)
  Pallas kernels: 73.6 us -> 69.2 us
    pallas_call x1, Pallas kernels: 73.6 us -> 69.2 us  [body(): pl.pallas_call(kernel, out_shape=jax.ShapeDtypeStruct(local, F32), in_spe...]
where the time goes in v3:
time: 71 us; the launch traced here: 70.9 us
  Pallas kernels  69.2 us (97%)
  other arithmetic  1.68 us (2%)
    pallas_call x1, Pallas kernels, body(): pl.pallas_call(kernel, out_shape=jax.ShapeDtypeStruct(local, F32), in_spe...  69.2 us
    broadcast_in_dim x1, other arithmetic, body(): return (initial + correction)[None]  1.68 us

profile of v3, /device:TPU:1, one launch (start us, length us, event | category | flops | bytes accessed | tf_op | source)
XLA Modules:
  0.0 70.9 jit_solution(14131116485386825028)
XLA Ops:
  0.0 0.0 copy-start
  0.0 69.2 %shard_map.55 = f32[4,128,128]{2,1,0:T(8,128)} custom-call(f32[4,128,128]{2,1,0:T(8,128)} %bitcast.3, f32[4,128,128]{2,1,0:T(8,128)} %initial.1, f32[4,128,128]{2,1,0:T(8,128)} %coupling.1, f32[3,4,128,128]{3,2,1,0:T(8,128)} %velocity.1, f32[4,5,8,128]{3,2,1,0:T(8,128)} %constant.2.clone.table_in), custom_call_target="tpu_custom_call" | custom-call | tf_op jit(solution)/shard_map/pallas_call | solution.py:564
  69.2 0.0 copy-done
  69.2 1.7 %add_bitcast_fusion = f32[1,4,128,128]{3,2,1,0:T(8,128)} fusion(f32[4,128,128]{2,1,0:T(8,128)S(1)} %copy-done, f32[4,128,128]{2,1,0:T(8,128)} %shard_map.55), kind=kLoop, calls=%fused_computation | loop fusion | flops 65536 | bytes 786432 | tf_op jit(solution)/shard_map/broadcast_in_dim | solution.py:601
Async XLA Ops:
  0.0 69.2 %copy-start = (f32[4,128,128]{2,1,0:T(8,128)S(1)}, f32[4,128,128]{2,1,0:T(8,128)}, u32[]{:S(2)}) copy-start(f32[4,128,128]{2,1,0:T(8,128)} %initial.1) | copy-start | bytes 786436

commit v4 on v3

--- a/solution.py
+++ b/solution.py
@@ -102,7 +102,7 @@
     r, along = lax.rem(m, 4), lax.div(m, 4)
     x = r + lax.rem(along, 2) * (3 - 2 * r)
     return (
-        lax.rem(x, 2) * 16 + along * 2 + lax.rem(zz, 2),
+        lax.rem(x, 2) * 16 + along * 2 + lax.rem(zz + m + 2, 2),
         lax.div(zz, 2) * 2 + lax.div(x, 2),
     )
 
@@ -149,8 +149,9 @@
     x = 2 * x_hi + lax.div(me_t, 16)
     r = x + lax.rem(along, 2) * (3 - 2 * x)
     m = along * 4 + r
-    zz = row * 2 + core
-    swap = lax.rem(core + x_hi, 2)
+    half = lax.rem(core + m, 2)
+    zz = row * 2 + half
+    swap = lax.rem(half + x_hi, 2)
     target = m + swap * (3 - 2 * r)
     x_lo = x - 2 * x_hi
 
@@ -215,7 +216,7 @@
 
         @pl.when(swap == 1 if mine else True)
         def _():
-            pl.semaphore_signal(barrier, inc=1, device_id=(t, row * 2 + core), device_id_type=MESH)
+            pl.semaphore_signal(barrier, inc=1, device_id=(t, row * 2 + half), device_id_type=MESH)
 
     for side in range(8):
 
@@ -245,7 +246,7 @@
         for to_x in range(4):
             chunk = 4 * zs[step] + xs[to_x] + turned[step] * (3 - 2 * xs[to_x])
             to = (
-                (xs[to_x] - 2 * x_his[to_x]) * 16 + zs[step] * 2 + x_hi,
+                (xs[to_x] - 2 * x_his[to_x]) * 16 + zs[step] * 2 + lax.rem(x_hi + chunk, 2),
                 row * 2 + x_his[to_x],
             )
 
@@ -293,7 +294,7 @@
         dst_ref=own_params,
         send_sem=param_send,
         recv_sem=param_recv,
-        device_id=device_at(target, row * 2 + 1 - core),
+        device_id=device_at(target, row * 2 + 1 - half),
         device_id_type=MESH,
     )
     @pl.when(swap == 1)
@@ -403,21 +404,23 @@
         return pltpu.make_async_remote_copy(
             src_ref=refs[0],
             dst_ref=refs[1],
-            send_sem=halo_send.at[g, parity],
-            recv_sem=halo_recv.at[g, parity],
+            send_sem=halo_send.at[g, parity, side // 4],
+            recv_sem=halo_recv.at[g, parity, side // 4],
             device_id=side_device[side],
             device_id_type=MESH,
         )
 
+    corners_first = (4, 5, 6, 7, 0, 1, 2, 3)
+
     def halo_start(g, parity):
         @pl.when(interior)
         def _():
-            for side in range(8):
+            for side in corners_first:
                 halo_copy(g, parity, side).start()
 
         @pl.when(jnp.logical_not(interior))
         def _():
-            for side in range(8):
+            for side in corners_first:
 
                 @pl.when(has[side])
                 def _():
@@ -425,21 +428,21 @@
 
     whole_y, whole_z = jnp.logical_and(has[0], has[1]), jnp.logical_and(has[2], has[3])
 
-    def halo_wait(g, parity):
+    def halo_wait(g, parity, corners):
         for tiles, when in (
-            (36, interior),
-            (26, whole_y != whole_z),
-            (17, jnp.logical_not(jnp.logical_or(whole_y, whole_z))),
+            ((32, 4), interior),
+            ((24, 2), whole_y != whole_z),
+            ((16, 1), jnp.logical_not(jnp.logical_or(whole_y, whole_z))),
         ):
 
             @pl.when(when)
             def _():
-                amount = spread.at[pl.ds(0, tiles * 8)]
+                amount = spread.at[pl.ds(0, tiles[corners] * 8)]
                 pltpu.make_async_remote_copy(
                     src_ref=amount,
                     dst_ref=amount,
-                    send_sem=halo_send.at[g, parity],
-                    recv_sem=halo_recv.at[g, parity],
+                    send_sem=halo_send.at[g, parity, corners],
+                    recv_sem=halo_recv.at[g, parity, corners],
                     device_id=(me_t, me_s),
                     device_id_type=MESH,
                 ).wait()
@@ -471,15 +474,21 @@
     ring = ring + [(-1, i) for i in range(4)] + [(4, i) for i in range(4)]
     ring = ring[4:8] + ring[0:4] + ring[12:16] + ring[8:12]
 
+    plain = [16 + i for i in range(16) if i % 4 in (1, 2)]
+    beside = [16 + i for i in range(16) if i % 4 in (0, 3)]
+
     def two_sweeps(g, parity, send):
-        halo_wait(g, parity)
         old, new = d.at[g, parity], d.at[g, 1 - parity]
-        for at in range(32):
-            z, y = (at // 4, at % 4) if at < 16 else ring[at - 16]
-            v = divide(g, at, stencil(old, z + 2, y + 2, at))
-            middle_d[z + 1, y + 1] = v
-            if at < 16:
-                total[pl.ds(at * 32 + g * 8, 8)] += v
+        halo_wait(g, parity, 0)
+        for cells in (list(range(16)) + plain, beside):
+            if cells is beside:
+                halo_wait(g, parity, 1)
+            for at in cells:
+                z, y = (at // 4, at % 4) if at < 16 else ring[at - 16]
+                v = divide(g, at, stencil(old, z + 2, y + 2, at))
+                middle_d[z + 1, y + 1] = v
+                if at < 16:
+                    total[pl.ds(at * 32 + g * 8, 8)] += v
         for at in range(16):
             z, y = at // 4, at % 4
             v = divide(g, at, stencil(middle_d, z + 1, y + 1, at))
@@ -500,7 +509,8 @@
             s += table[g, 3] * total[pl.ds(p * 32 + g * 8, 8)]
         wrap[p] = jnp.broadcast_to(jnp.sum(s, axis=0, keepdims=True), (8, 128))
     for g in range(GROUPS):
-        halo_wait(g, 0)
+        halo_wait(g, 0, 0)
+        halo_wait(g, 0, 1)
         for at in range(16):
             z, y = at // 4, at % 4
             s = stencil(d.at[g, 0], z + 2, y + 2, at) - table[g, 4] * wrap[at]
@@ -534,7 +544,7 @@
                 dst_ref=gathered.at[m],
                 send_sem=back_send,
                 recv_sem=back_recv,
-                device_id=(t, row * 2 + core),
+                device_id=(t, row * 2 + half),
                 device_id_type=MESH,
             ).start()
 
@@ -563,7 +573,7 @@
     dma = pltpu.SemaphoreType.DMA
     correction = pl.pallas_call(
         kernel,
-        out_shape=jax.ShapeDtypeStruct(local, F32),
+        out_shape=pltpu.VMEM(local, F32),
         in_specs=[hbm] * 5,
         out_specs=pl.BlockSpec(memory_space=pltpu.VMEM),
         scratch_shapes=[
@@ -593,8 +603,8 @@
             dma,
             dma((4,)),
             dma((4,)),
-            dma((GROUPS, 2)),
-            dma((GROUPS, 2)),
+            dma((GROUPS, 2, 2)),
+            dma((GROUPS, 2, 2)),
         ],
         compiler_params=pltpu.CompilerParams(collective_id=0, has_side_effects=True),
     )(forcing[0], initial, coupling, velocity, table)

time: 71 us -> 65 us (0.915)
  Pallas kernels: 69.2 us -> 63.7 us
  other arithmetic: 1.68 us -> 0.73 us
    pallas_call x1, Pallas kernels: 69.2 us -> 63.7 us  [body(): pl.pallas_call(kernel, out_shape=pltpu.VMEM(local, F32), in_specs=[hbm] *...]
    broadcast_in_dim x1, other arithmetic: 1.68 us -> 0.73 us  [body(): return (initial + correction)[None]]
where the time goes in v4:
time: 65 us; the launch traced here: 64.4 us
  Pallas kernels  63.7 us (98%)
  other arithmetic  0.73 us (1%)
    pallas_call x1, Pallas kernels, body(): pl.pallas_call(kernel, out_shape=pltpu.VMEM(local, F32), in_specs=[hbm] *...  63.7 us

profile of v4, /device:TPU:1, one launch (start us, length us, event | category | flops | bytes accessed | tf_op | source)
XLA Modules:
  0.0 64.4 jit_solution(4353345065920530818)
XLA Ops:
  0.0 0.0 copy-start
  0.0 63.7 %shard_map.55 = f32[4,128,128]{2,1,0:T(8,128)S(1)} custom-call(f32[4,128,128]{2,1,0:T(8,128)} %bitcast.3, f32[4,128,128]{2,1,0:T(8,128)} %initial.1, f32[4,128,128]{2,1,0:T(8,128)} %coupling.1, f32[3,4,128,128]{3,2,1,0:T(8,128)} %velocity.1, f32[4,5,8,128]{3,2,1,0:T(8,128)} %constant.2.clone.table_in), custom_call_target="tpu_custom_call" | custom-call | tf_op jit(solution)/shard_map/pallas_call | solution.py:574
  63.7 0.0 copy-done
  63.7 0.7 %add_bitcast_fusion = f32[1,4,128,128]{3,2,1,0:T(8,128)} fusion(f32[4,128,128]{2,1,0:T(8,128)S(1)} %copy-done, f32[4,128,128]{2,1,0:T(8,128)S(1)} %shard_map.55), kind=kLoop, calls=%fused_computation | loop fusion | flops 65536 | bytes 786432 | tf_op jit(solution)/shard_map/broadcast_in_dim | solution.py:611
Async XLA Ops:
  0.0 63.7 %copy-start = (f32[4,128,128]{2,1,0:T(8,128)S(1)}, f32[4,128,128]{2,1,0:T(8,128)}, u32[]{:S(2)}) copy-start(f32[4,128,128]{2,1,0:T(8,128)} %initial.1) | copy-start | bytes 786436

commit v5 on v4

--- a/solution.py
+++ b/solution.py
@@ -204,13 +204,13 @@
 
     count = 31 + swap
     def senders():
-        for step in far_first:
-            for flip_x in range(2):
-                for flip_core in range(2):
-                    to_x = 1 - x_lo if flip_x else x_lo
-                    to_core = 1 - core if flip_core else core
-                    t = to_x * 16 + zs[step] * 2 + to_core
-                    yield t, step == 0 and flip_x == 0 and flip_core == 0
+        order = [(step, near) for step in far_first for near in range(2)]
+        for step, near in sorted(order, key=lambda at: at[1] - min(at[0], 8 - at[0])):
+            flip = swap if near else 1 - swap
+            to_x = x_lo + flip - 2 * x_lo * flip
+            for to_core in (1 - core, core):
+                mine = step == 0 and near == 1 and to_core is core
+                yield to_x * 16 + zs[step] * 2 + to_core, mine
 
     for t, mine in senders():
 

time: 65 us -> 65 us (level)
  no operation moved by 1% of the time
where the time goes in v5:
time: 65 us; the launch traced here: 64.4 us
  Pallas kernels  63.6 us (98%)
  other arithmetic  0.73 us (1%)
    pallas_call x1, Pallas kernels, body(): pl.pallas_call(kernel, out_shape=pltpu.VMEM(local, F32), in_specs=[hbm] *...  63.6 us

profile of v5, /device:TPU:1, one launch (start us, length us, event | category | flops | bytes accessed | tf_op | source)
XLA Modules:
  0.0 64.4 jit_solution(4280708289763535394)
XLA Ops:
  0.0 0.0 copy-start
  0.0 63.6 %shard_map.55 = f32[4,128,128]{2,1,0:T(8,128)S(1)} custom-call(f32[4,128,128]{2,1,0:T(8,128)} %bitcast.3, f32[4,128,128]{2,1,0:T(8,128)} %initial.1, f32[4,128,128]{2,1,0:T(8,128)} %coupling.1, f32[3,4,128,128]{3,2,1,0:T(8,128)} %velocity.1, f32[4,5,8,128]{3,2,1,0:T(8,128)} %constant.2.clone.table_in), custom_call_target="tpu_custom_call" | custom-call | tf_op jit(solution)/shard_map/pallas_call | solution.py:574
  63.7 0.0 copy-done
  63.7 0.7 %add_bitcast_fusion = f32[1,4,128,128]{3,2,1,0:T(8,128)} fusion(f32[4,128,128]{2,1,0:T(8,128)S(1)} %copy-done, f32[4,128,128]{2,1,0:T(8,128)S(1)} %shard_map.55), kind=kLoop, calls=%fused_computation | loop fusion | flops 65536 | bytes 786432 | tf_op jit(solution)/shard_map/broadcast_in_dim | solution.py:611
Async XLA Ops:
  0.0 63.7 %copy-start = (f32[4,128,128]{2,1,0:T(8,128)S(1)}, f32[4,128,128]{2,1,0:T(8,128)}, u32[]{:S(2)}) copy-start(f32[4,128,128]{2,1,0:T(8,128)} %initial.1) | copy-start | bytes 786436
